TPU v7x, 8 devices: a whole 2x2x1 slice. The times are simulated.
8 devices in a mesh: dp: 1 (over z), sp: 8 (over y, x, core).
Axes of the slice: x: 2, y: 2, z: 1, core: 2. Of those that a mesh axis runs over, the one named last changes fastest.
Arguments:
- hidden: bfloat16 [128, 6144], P('dp')
- ln_gamma: float32 [6144], replicated
- ln_beta: float32 [6144], replicated
- w_qkv: bfloat16 [6144, 6400], replicated
- w_out: bfloat16 [6144, 6144], replicated
- w_up: bfloat16 [6144, 24576], P(None, 'sp')
- w_down: bfloat16 [24576, 6144], P('sp')
- k_cache: bfloat16 [128, 4096, 128], P('dp', 'sp')
- v_cache: bfloat16 [128, 4096, 128], P('dp', 'sp')
- positions: int32 [128], P('dp')
Outputs:
- output 1: bfloat16 [128, 6144], P('dp')
- output 2: bfloat16 [128, 4096, 128], P('dp', 'sp')
- output 3: bfloat16 [128, 4096, 128], P('dp', 'sp')
All inputs are finite; a program needn't handle non-finite values.
Results may differ from a plain program's by a relative error of at most 0.00574734.
Values sent between devices are 32-bit elements.
A program may use at most 1.25 GiB of HBM per device.

v0:
```python
import jax
import jax.numpy as jnp
from jax import lax
from jax.sharding import PartitionSpec as P

LN_EPS = 1e-5
ROPE_BASE = 10000.0
NEG_FILL = -1e30


def layer_norm(hidden, ln_gamma, ln_beta):
    hidden_f32 = hidden.astype(jnp.float32)
    row_mean = jnp.mean(hidden_f32, axis=-1, keepdims=True)
    centered = hidden_f32 - row_mean
    row_var = jnp.mean(centered * centered, axis=-1, keepdims=True)
    return (centered * lax.rsqrt(row_var + LN_EPS) * ln_gamma + ln_beta).astype(jnp.bfloat16)


def rotary_tables(positions, head_dim):
    inv_freq = 1.0 / (ROPE_BASE ** (jnp.arange(0, head_dim, 2, dtype=jnp.float32) / head_dim))
    angles = positions.astype(jnp.float32)[:, None] * inv_freq[None, :]
    cos_half = jnp.cos(angles)
    sin_half = jnp.sin(angles)
    return jnp.concatenate([cos_half, cos_half], axis=-1), jnp.concatenate([sin_half, sin_half], axis=-1)


def apply_rotary(vecs, cos_full, sin_full):
    vecs_f32 = vecs.astype(jnp.float32)
    half_dim = vecs.shape[-1] // 2
    rotated = jnp.concatenate([-vecs_f32[..., half_dim:], vecs_f32[..., :half_dim]], axis=-1)
    return (vecs_f32 * cos_full + rotated * sin_full).astype(jnp.bfloat16)


def local_stats(q_rot, k_block, v_block, local_pos):
    head_dim = q_rot.shape[-1]
    slot_ids = jnp.arange(k_block.shape[1])
    scores = jnp.einsum('bhd,bsd->bhs', q_rot, k_block, preferred_element_type=jnp.float32) * head_dim ** -0.5
    valid_mask = (slot_ids[None, :] <= local_pos[:, None])[:, None, :]
    masked = jnp.where(valid_mask, scores, NEG_FILL)
    block_max = jnp.max(masked, axis=-1)
    exp_scores = jnp.where(valid_mask, jnp.exp(masked - block_max[..., None]), 0.0)
    block_sum = jnp.sum(exp_scores, axis=-1)
    block_ctx = jnp.einsum('bhs,bsd->bhd', exp_scores.astype(jnp.bfloat16), v_block, preferred_element_type=jnp.float32)
    return jnp.concatenate([block_ctx, block_max[..., None], block_sum[..., None]], axis=-1)


def combine_stats(all_stats):
    head_dim = all_stats.shape[-1] - 2
    block_max = all_stats[..., head_dim]
    top_max = jnp.max(block_max, axis=0)
    scale_w = jnp.exp(block_max - top_max[None])
    total_sum = jnp.sum(all_stats[..., head_dim + 1] * scale_w, axis=0)
    total_ctx = jnp.sum(all_stats[..., :head_dim] * scale_w[..., None], axis=0)
    return (total_ctx / total_sum[..., None]).astype(jnp.bfloat16)


def device_step(hidden, ln_gamma, ln_beta, w_qkv, w_out, w_up, w_down, k_cache, v_cache, positions):
    batch_rows = hidden.shape[0]
    seq_dev, head_dim = k_cache.shape[1], k_cache.shape[2]
    num_heads = w_out.shape[0] // head_dim
    normed = layer_norm(hidden, ln_gamma, ln_beta)
    qkv_proj = jnp.dot(normed, w_qkv, preferred_element_type=jnp.float32).astype(jnp.bfloat16)
    qkv_proj = qkv_proj.reshape(batch_rows, num_heads + 2, head_dim)
    cos_full, sin_full = rotary_tables(positions, head_dim)
    q_rot = apply_rotary(qkv_proj[:, :num_heads], cos_full[:, None, :], sin_full[:, None, :])
    k_rot = apply_rotary(qkv_proj[:, num_heads], cos_full, sin_full)
    v_new = qkv_proj[:, num_heads + 1]
    local_pos = positions - lax.axis_index('sp') * seq_dev
    write_mask = (jnp.arange(seq_dev)[None, :] == local_pos[:, None])[:, :, None]
    k_next = jnp.where(write_mask, k_rot[:, None, :], k_cache)
    v_next = jnp.where(write_mask, v_new[:, None, :], v_cache)
    block_stats = local_stats(q_rot, k_next, v_next, local_pos)
    all_stats = lax.all_gather(block_stats, 'sp')
    context = combine_stats(all_stats).reshape(batch_rows, num_heads * head_dim)
    attn_out = jnp.dot(context, w_out, preferred_element_type=jnp.float32)
    up_proj = jnp.dot(normed, w_up, preferred_element_type=jnp.float32)
    activated = jax.nn.gelu(up_proj, approximate=False).astype(jnp.bfloat16)
    mlp_part = jnp.dot(activated, w_down, preferred_element_type=jnp.float32)
    mlp_out = lax.psum(mlp_part, 'sp')
    out_hidden = (hidden.astype(jnp.float32) + attn_out + mlp_out).astype(jnp.bfloat16)
    return out_hidden, k_next, v_next


def solution(mesh):
    cache_spec = P('dp', 'sp', None)
    in_specs = (P('dp', None), P(None), P(None), P(None, None), P(None, None), P(None, 'sp'), P('sp', None), cache_spec, cache_spec, P('dp'))
    out_specs = (P('dp', None), cache_spec, cache_spec)
    return jax.shard_map(device_step, mesh=mesh, in_specs=in_specs, out_specs=out_specs, check_vma=False)
```

profile of v0, /device:TPU:0, one launch (start us, length us, event | category | flops | bytes accessed | tf_op | source)
XLA Modules:
  0.0 349.0 jit_solution(16499565794674292248)
XLA Ops:
  7.3 0.8 broadcast_subtract_fusion
  8.0 0.2 fusion.70
  8.2 0.2 multiply_cosine_fusion.1
  8.4 1.7 convert_reduce_fusion
  10.1 2.0 fusion.15
  12.2 27.8 %convolution_convert_fusion = bf16[128,6400]{1,0:T(8,128)(2,1)} fusion(bf16[6144,6400]{1,0:T(8,128)(2,1)} %param.13, bf16[128,6144]{1,0:T(8,128)(2,1)S(1)} %copy-done.1, f32[6144]{0:T(1024)S(1)} %copy-done.2, f32[6144]{0:T(1024)S(1)} %copy-done.3, f32[128]{0:T(128)S(1)} %add_rsqrt_fusion, f32[128]{0:T(128)S(1)} %broadcast_multiply_fusion), kind=kOutput, calls=%fused_computation.9 | convolution fusion | flops 10071867392 | bytes 81904640 | tf_op jit(solution)/shard_map/dot_general | solution.py:62
  40.0 2.9 copy.60
  42.9 2.0 slice_convert_fusion
  45.0 0.1 copy.61
  45.1 0.1 copy.63
  45.2 0.2 iota_compare_fusion.1
  45.4 2.2 slice_negate_fusion
  47.5 1.7 fusion.20
  49.3 2.0 copy.62
  51.3 23.3 %broadcast_select_fusion = (bf16[128,512,128]{2,1,0:T(8,128)(2,1)}, bf16[128,512,128]{2,1,0:T(8,128)(2,1)}) fusion(bf16[128,512,128]{2,1,0:T(8,128)(2,1)} %param.18, pred[128,512]{1,0:T(8,128)(4,1)S(1)} %get-tuple-element.15, bf16[128,128]{1,0:T(8,128)(2,1)S(1)} %bitcast.55, bf16[128,512,128]{2,1,0:T(8,128)(2,1)} %param.17, bf16[128,128]{1,0:T(8,128)(2,1)S(1)} %copy.61), kind=kLoop, calls=%fused_computation.2 | loop fusion | flops 16777216 | bytes 67239936 | tf_op jit(solution)/shard_map/jit(_where)/select_n | solution.py:71
  74.6 12.2 %fusion.1 = (f32[128,48]{1,0:T(8,128)S(1)}, f32[128,48,512]{2,1,0:T(8,128)}) fusion(pred[128,512]{1,0:T(8,128)(4,1)S(1)} %get-tuple-element.14, bf16[128,48,128]{2,1,0:T(8,128)(2,1)S(1)} %copy.62, bf16[128,512,128]{2,1,0:T(8,128)(2,1)} %get-tuple-element.8), kind=kOutput, calls=%fused_computation.6 | convolution fusion | flops 814737408 | bytes 31023104 | tf_op jit(solution)/shard_map/bhd,bsd->bhs/dot_general | solution.py:37
  86.8 9.4 %fusion.2 = f32[128,48]{1,0:T(8,128)S(1)} fusion(f32[128,48,512]{2,1,0:T(8,128)} %get-tuple-element.19, f32[128,48]{1,0:T(8,128)S(1)} %get-tuple-element.18, pred[128,512]{1,0:T(8,128)(4,1)S(1)} %get-tuple-element.14), kind=kLoop, calls=%fused_computation.7 | loop fusion | flops 15722496 | bytes 12697600 | tf_op jit(solution)/shard_map/reduce_sum | solution.py:42
  96.2 8.9 %fusion.6 = f32[128,48,128]{2,1,0:T(8,128)} fusion(bf16[128,512,128]{2,1,0:T(8,128)(2,1)} %get-tuple-element.7, f32[128,48,512]{2,1,0:T(8,128)S(1)} %copy-done, f32[128,48]{1,0:T(8,128)S(1)} %get-tuple-element.18, pred[128,512]{1,0:T(8,128)(4,1)S(1)} %get-tuple-element.14), kind=kOutput, calls=%fused_computation.13 | convolution fusion | flops 821035008 | bytes 32595968 | tf_op jit(solution)/shard_map/bhs,bsd->bhd/dot_general | solution.py:43
  105.1 2.4 copy.67
  107.5 2.3 copy.66
  109.7 7.7 %pad_maximum_fusion = f32[128,48,130]{2,1,0:T(8,128)} fusion(f32[128,48,1]{2,1,0:T(8,128)} %copy.67, f32[128,48,1]{2,1,0:T(8,128)} %copy.66, f32[128,48,128]{2,1,0:T(8,128)} %fusion.6), kind=kLoop, calls=%fused_computation.14 | loop fusion | flops 1597440 | bytes 6389760 | tf_op jit(solution)/shard_map/concatenate | solution.py:44
  117.4 6.1 %copy.68 = f32[128,48,130]{0,1,2:T(8,128)} copy(f32[128,48,130]{2,1,0:T(8,128)} %pad_maximum_fusion) | data formatting | bytes 6389760 | tf_op jit(solution)/shard_map/concatenate | solution.py:44
  123.6 29.1 %fusion.31 = f32[128,6144]{1,0:T(8,128)} fusion(bf16[3072,6144]{1,0:T(8,128)(2,1)} %param.16, bf16[6144,3072]{1,0:T(8,128)(2,1)} %param.15, bf16[128,6144]{1,0:T(8,128)(2,1)S(1)} %copy-done.1, f32[6144]{0:T(1024)S(1)} %copy-done.2, f32[6144]{0:T(1024)S(1)} %copy-done.3, f32[128]{0:T(128)S(1)} %add_rsqrt_fusion, f32[128]{0:T(128)S(1)} %broadcast_multiply_fusion), kind=kOutput, calls=%fused_computation.53 | convolution fusion | flops 9693954048 | bytes 80266240 | tf_op jit(solution)/shard_map/dot_general | solution.py:78
  152.7 100.2 %all-gather.3.cloned.1.call-done = f32[1024,48,130]{0,1,2:T(8,128)} async-done(((f32[128,48,130]{0,1,2:T(8,128)}), f32[1024,48,130]{0,1,2:T(8,128)}) %all-gather.3.cloned.1.call-update) | async-done | bytes 25559056 | tf_op jit(solution)/shard_map/all_gather | solution.py:73
  252.9 13.5 %copy.79 = f32[780,8,8,128]{3,2,1,0:T(8,128)S(1)} copy(f32[780,8,8,128]{3,1,2,0:T(8,128)} %bitcast.47) | data formatting | bytes 51118080
  266.4 0.1 slice_reduce_fusion
  266.4 0.1 fusion.64
  266.6 25.8 %fusion = f32[128,48,128]{0,1,2:T(8,128)S(1)} fusion(f32[8,128,48,130]{1,0,2,3:T(8,128)S(1)} %bitcast.46, f32[8,128,48]{1,0,2:T(8,128)S(1)} %exponential_bitcast_fusion), kind=kLoop, calls=%fused_computation.1 | loop fusion | flops 11796480 | bytes 28508160 | tf_op jit(solution)/shard_map/reduce_sum | solution.py:53
  292.4 0.3 divide_convert_fusion
  292.6 0.4 copy.72
  293.1 21.2 %all-reduce.2.cloned.1.call-done = f32[128,6144]{1,0:T(8,128)} async-done(((f32[128,6144]{1,0:T(8,128)}), f32[128,6144]{1,0:T(8,128)}) %all-reduce.2.cloned.1.call-update) | async-done | bytes 3145744 | tf_op jit(solution)/shard_map/psum | solution.py:79
  314.2 27.9 %fusion.5 = bf16[128,6144]{1,0:T(8,128)(2,1)} fusion(f32[128,6144]{1,0:T(8,128)} %all-reduce.2.cloned.1.call-done, bf16[128,6144]{0,1:T(8,128)(2,1)S(1)} %bitcast.52, bf16[6144,6144]{1,0:T(8,128)(2,1)} %param.14, bf16[128,6144]{1,0:T(8,128)(2,1)S(1)} %copy-done.1), kind=kOutput, calls=%fused_computation.12 | convolution fusion | flops 9666822144 | bytes 83361792 | tf_op jit(solution)/shard_map/dot_general | solution.py:75
  (20 shorter events, 0.2 us)
Async XLA Ops:
  7.2 5.0 %copy-start.1 = (bf16[128,6144]{1,0:T(8,128)(2,1)S(1)}, bf16[128,6144]{1,0:T(8,128)(2,1)}, u32[]{:S(2)}) copy-start(bf16[128,6144]{1,0:T(8,128)(2,1)} %param.10) | copy-start | bytes 4718596
  7.2 5.0 %copy-start.3 = (f32[6144]{0:T(1024)S(1)}, f32[6144]{0:T(1024)}, u32[]{:S(2)}) copy-start(f32[6144]{0:T(1024)} %param.11) | copy-start | bytes 73732
  7.2 5.0 %copy-start.2 = (f32[6144]{0:T(1024)S(1)}, f32[6144]{0:T(1024)}, u32[]{:S(2)}) copy-start(f32[6144]{0:T(1024)} %param.12) | copy-start | bytes 73732
  7.2 245.7 %all-gather.3.cloned.1.call-start = ((), (), s32[]{:S(2)}) async-start(), calls=%async_computation.1 | async-start | bytes 28753920 | tf_op jit(solution)/shard_map/all_gather | solution.py:73
  86.8 9.4 %copy-start = (f32[128,48,512]{2,1,0:T(8,128)S(1)}, f32[128,48,512]{2,1,0:T(8,128)}, u32[]{:S(2)}) copy-start(f32[128,48,512]{2,1,0:T(8,128)} %get-tuple-element.19) | copy-start | bytes 37748740
  123.5 190.7 %all-reduce.2.cloned.1.call-start = ((), (), s32[]{:S(2)}) async-start(), calls=%async_computation | async-start | bytes 6291456 | tf_op jit(solution)/shard_map/psum | solution.py:79
Sparse Core Ops, SparseCore 0:
  123.6 129.2 all-gather.2
  256.2 58.0 all-reduce.1
where the time goes:
time: 349 us
  waiting for transfers between devices  121 us (35%)
  matrix products  106 us (30%)
  other arithmetic  77.6 us (22%)
  local copies, waits for them, and re-layouts  29.8 us (9%)
  between operations  14.3 us (4%)
    all_gather x1, waiting for transfers between devices, device_step(): all_stats = lax.all_gather(block_stats, 'sp')  100 us
    dot_general x1, matrix products, device_step(): mlp_part = jnp.dot(activated, w_down, preferred_element_type=jnp.float32)  29.1 us
    dot_general x1, matrix products, device_step(): attn_out = jnp.dot(context, w_out, preferred_element_type=jnp.float32)  27.9 us
    dot_general x1, matrix products, device_step(): jnp.dot(normed, w_qkv, preferred_element_type=jnp.float32)  27.8 us
    reduce_sum x1, other arithmetic, combine_stats(): total_ctx = jnp.sum(all_stats[..., :head_dim] * scale_w[..., None], axis=0)  25.8 us
    select_n x1, other arithmetic, device_step(): v_next = jnp.where(write_mask, v_new[:, None, :], v_cache)  23.3 us
    psum x1, waiting for transfers between devices, device_step(): mlp_out = lax.psum(mlp_part, 'sp')  21.2 us
    unnamed x9, local copies, waits for them, and re-layouts  13.5 us
  transfers between devices with their start and end apart: 2, of which 2 were waited for; matrix products, arithmetic and copies ran while one was open for 20% of the time, Pallas kernels for 0%

commit v1 on v0

v1 whole, which is shorter than its diff:
```python
import functools

import jax
import jax.numpy as jnp
from jax import lax
from jax.experimental import pallas as pl
from jax.experimental.pallas import tpu as pltpu
from jax.sharding import PartitionSpec as P

LN_EPS = 1e-5
ROPE_BASE = 10000.0
NEG_FILL = -1e30
MESH = pl.DeviceIdType.MESH
VMEM_LIMIT = 67_000_000

ROWS = 128
D = 6144
HD = 128
NH = 48
SEQ = 512
FF = 3072
F32 = jnp.float32
BF16 = jnp.bfloat16


def rotary_tables(positions):
    inv_freq = 1.0 / (ROPE_BASE ** (jnp.arange(0, HD, 2, dtype=F32) / HD))
    angles = positions.astype(F32)[:, None] * inv_freq[None, :]
    cos_half = jnp.cos(angles)
    sin_half = jnp.sin(angles)
    return jnp.concatenate([cos_half, cos_half], axis=-1), jnp.concatenate([-sin_half, sin_half], axis=-1)


def place():
    sp = lax.axis_index('sp')
    core = lax.rem(sp, 2)
    x = lax.rem(sp // 2, 2)
    y = sp // 4
    return y, x, core


def device(y, x, core):
    return {'sp': (y * 2 + x) * 2 + core}


def enter(peers):
    barrier = pltpu.get_barrier_semaphore()
    for peer in peers:
        pl.semaphore_signal(barrier, inc=1, device_id=peer, device_id_type=MESH)
    pl.semaphore_wait(barrier, len(peers))


Q_BLOCK = 640
Q_STEPS = 5
Q_SLOTS = 6


def qkv_kernel(hid, gam, bet, cos, sin, w, qkv, normed, wbuf, mine, wsem, lsem, ssem, rsem):
    y, x, core = place()
    partner = device(y, x, 1 - core)

    def fetch(j, half):
        col = pl.multiple_of(core * 3200 + j * Q_BLOCK, 128)
        slot = lax.rem(2 * j + half, Q_SLOTS)
        return pltpu.make_async_copy(w.at[pl.ds(half * 3072, 3072), pl.ds(col, Q_BLOCK)], wbuf.at[slot], wsem.at[slot])

    for j in range(Q_SLOTS // 2):
        fetch(j, 0).start()
        fetch(j, 1).start()
    enter([partner])

    def norm_rows(i, carry):
        rows = pl.ds(pl.multiple_of(i * 16, 16), 16)
        v = hid[rows, :].astype(F32)
        mean = jnp.sum(v, axis=-1, keepdims=True) * (1.0 / D)
        cen = v - mean
        var = jnp.sum(cen * cen, axis=-1, keepdims=True) * (1.0 / D)
        normed[rows, :] = (cen * lax.rsqrt(var + LN_EPS) * gam[...] + bet[...]).astype(BF16)
        return carry

    lax.fori_loop(0, ROWS // 16, norm_rows, 0)

    def remote(j):
        return pltpu.make_async_remote_copy(
            src_ref=mine.at[pl.ds(j * 5, 5)], dst_ref=qkv.at[pl.ds(core * 25 + j * 5, 5)],
            send_sem=ssem.at[j], recv_sem=rsem.at[j], device_id=partner, device_id_type=MESH)

    def local(j):
        return pltpu.make_async_copy(mine.at[pl.ds(j * 5, 5)], qkv.at[pl.ds(core * 25 + j * 5, 5)], lsem.at[j])

    def block(j, carry):
        fetch(j, 0).wait()
        fetch(j, 1).wait()
        s0 = lax.rem(2 * j, Q_SLOTS)
        acc = jnp.dot(normed[:, :3072], wbuf[s0], preferred_element_type=F32)
        acc += jnp.dot(normed[:, 3072:], wbuf[s0 + 1], preferred_element_type=F32)

        @pl.when(j < Q_STEPS - Q_SLOTS // 2)
        def _():
            fetch(j + Q_SLOTS // 2, 0).start()
            fetch(j + Q_SLOTS // 2, 1).start()

        for h in range(5):
            v = acc[:, h * HD:(h + 1) * HD].astype(BF16).astype(F32)
            rot = (v * cos[...] + pltpu.roll(v, 64, 1) * sin[...]).astype(BF16).astype(F32)
            if h == 4:
                rot = jnp.where(core * 25 + j * 5 + h == NH + 1, v, rot)
            mine[j * 5 + h] = rot
        remote(j).start()
        local(j).start()
        return carry

    lax.fori_loop(0, Q_STEPS, block, 0)

    def drain(j, carry):
        local(j).wait()
        remote(j).wait()
        return carry

    lax.fori_loop(0, Q_STEPS, drain, 0)


def qkv_call(hidden, gam, bet, cos, sin, w_qkv):
    vm = pl.BlockSpec(memory_space=pltpu.VMEM)
    anyspace = pl.BlockSpec(memory_space=pl.ANY)
    return pl.pallas_call(
        qkv_kernel,
        out_shape=(jax.ShapeDtypeStruct((NH + 2, ROWS, HD), F32), jax.ShapeDtypeStruct((ROWS, D), BF16)),
        in_specs=[vm, vm, vm, vm, vm, anyspace],
        out_specs=(anyspace, vm),
        scratch_shapes=[
            pltpu.VMEM((Q_SLOTS, 3072, Q_BLOCK), BF16),
            pltpu.VMEM((25, ROWS, HD), F32),
            pltpu.SemaphoreType.DMA((Q_SLOTS,)),
            pltpu.SemaphoreType.DMA((Q_STEPS,)),
            pltpu.SemaphoreType.DMA((Q_STEPS,)),
            pltpu.SemaphoreType.DMA((Q_STEPS,)),
        ],
        compiler_params=pltpu.CompilerParams(collective_id=0, has_side_effects=True, vmem_limit_bytes=VMEM_LIMIT),
        cost_estimate=pl.CostEstimate(flops=2 * ROWS * D * 3200, bytes_accessed=D * 6400, transcendentals=0),
        name='qkv',
    )(hidden, gam, bet, cos, sin, w_qkv)


A_ROWS = 8
A_STEPS = ROWS // A_ROWS
A_SLOTS = 4


def attn_kernel(lp_ref, qkv, kc, vc, o, ml, kn, vn, kbuf, vbuf, isem, osem):
    i = pl.program_id(0)

    def fetch(step):
        slot = lax.rem(step, A_SLOTS)
        rows = pl.ds(step * A_ROWS, A_ROWS)
        return (pltpu.make_async_copy(kc.at[rows], kbuf.at[slot], isem.at[0, slot]),
                pltpu.make_async_copy(vc.at[rows], vbuf.at[slot], isem.at[1, slot]))

    def flush(step):
        slot = lax.rem(step, A_SLOTS)
        rows = pl.ds(step * A_ROWS, A_ROWS)
        return (pltpu.make_async_copy(kbuf.at[slot], kn.at[rows], osem.at[0, slot]),
                pltpu.make_async_copy(vbuf.at[slot], vn.at[rows], osem.at[1, slot]))

    @pl.when(i == 0)
    def _():
        for s in range(2):
            for c in fetch(s):
                c.start()

    @pl.when(i >= 2)
    def _():
        for c in flush(i - 2):
            c.wait()

    @pl.when(i + 2 < A_STEPS)
    def _():
        for c in fetch(i + 2):
            c.start()

    for c in fetch(i):
        c.wait()
    slot = lax.rem(i, A_SLOTS)

    for r in range(A_ROWS):
        lp = lp_ref[i * A_ROWS + r]
        base = pl.multiple_of((jnp.clip(lp, 0, SEQ - 1) // 16) * 16, 16)
        hit = base + lax.broadcasted_iota(jnp.int32, (16, HD), 0) == lp
        for buf, src in ((kbuf, NH), (vbuf, NH + 1)):
            new = jnp.broadcast_to(qkv[src, r:r + 1, :], (16, HD))
            old = buf[slot, r, pl.ds(base, 16), :].astype(F32)
            buf[slot, r, pl.ds(base, 16), :] = jnp.where(hit, new, old).astype(BF16)

    lane = lax.broadcasted_iota(jnp.int32, (NH, HD), 1)
    mcol = jnp.zeros((NH, HD), F32)
    lcol = jnp.zeros((NH, HD), F32)
    for r in range(A_ROWS):
        lp = lp_ref[i * A_ROWS + r]
        q = qkv[0:NH, r, :].astype(BF16)
        s = lax.dot_general(q, kbuf[slot, r], (((1,), (1,)), ((), ())), preferred_element_type=F32) * (HD ** -0.5)
        valid = lax.broadcasted_iota(jnp.int32, (NH, SEQ), 1) <= lp
        s = jnp.where(valid, s, NEG_FILL)
        m = jnp.max(s, axis=-1, keepdims=True)
        e = jnp.where(valid, jnp.exp(s - m), 0.0)
        l = jnp.sum(e, axis=-1, keepdims=True)
        o[:, r, :] = jnp.dot(e.astype(BF16), vbuf[slot, r], preferred_element_type=F32)
        mcol = jnp.where(lane == r, m, mcol)
        lcol = jnp.where(lane == r, l, lcol)
    pad = jnp.zeros((16, HD), F32)
    ml[...] = jnp.transpose(jnp.concatenate([mcol, pad, lcol, pad], axis=0))[:A_ROWS]

    for c in flush(i):
        c.start()

    @pl.when(i == A_STEPS - 1)
    def _():
        for step in (i - 1, i):
            for c in flush(step):
                c.wait()


def attn_call(local_pos, qkv, k_cache, v_cache):
    anyspace = pl.BlockSpec(memory_space=pl.ANY)
    cache = jax.ShapeDtypeStruct((ROWS, SEQ, HD), BF16)
    return pl.pallas_call(
        attn_kernel,
        out_shape=(jax.ShapeDtypeStruct((NH, ROWS, HD), F32), jax.ShapeDtypeStruct((ROWS, HD), F32), cache, cache),
        grid_spec=pltpu.PrefetchScalarGridSpec(
            num_scalar_prefetch=1,
            grid=(A_STEPS,),
            in_specs=[pl.BlockSpec((NH + 2, A_ROWS, HD), lambda i, p: (0, i, 0)), anyspace, anyspace],
            out_specs=(pl.BlockSpec((NH, A_ROWS, HD), lambda i, p: (0, i, 0)), pl.BlockSpec((A_ROWS, HD), lambda i, p: (i, 0)),
                       anyspace, anyspace),
            scratch_shapes=[
                pltpu.VMEM((A_SLOTS, A_ROWS, SEQ, HD), BF16),
                pltpu.VMEM((A_SLOTS, A_ROWS, SEQ, HD), BF16),
                pltpu.SemaphoreType.DMA((2, A_SLOTS)),
                pltpu.SemaphoreType.DMA((2, A_SLOTS)),
            ]),
        compiler_params=pltpu.CompilerParams(vmem_limit_bytes=VMEM_LIMIT, dimension_semantics=('arbitrary',)),
        cost_estimate=pl.CostEstimate(flops=4 * ROWS * NH * SEQ * HD, bytes_accessed=8 * ROWS * SEQ * HD, transcendentals=0),
        name='attn',
    )(local_pos, qkv, k_cache, v_cache)


W_SLOTS = 8
UP_STEPS = 12
DOWN_STEPS = 12
NK = 2
CT = NH // NK


def tail_kernel(normed, hid, ml_in, o_hbm, w_up, w_down, w_out, out,
                wbuf, wobuf, act, part, mine, orecv0, orecv1, orecv2, ml0, mlr, precv0, precv1, precv2, gath, ctx,
                wsem, wosem, mysem, osend, orecv, msend, mrecv, psend, precv, gsend, grecv):
    y, x, core = place()
    first = 1 - core
    partner = device(y, x, 1 - core)
    x_peer = (y, 1 - x, core)
    y_peer = (1 - y, x, core)
    n1 = {'sp': jnp.where(core == 0, device(*x_peer)['sp'], device(*y_peer)['sp'])}
    n2 = {'sp': jnp.where(core == 0, device(*y_peer)['sp'], device(*x_peer)['sp'])}
    a = x * first + y * core
    b = y * first + x * core

    def fetch_up(step):
        slot = lax.rem(step, W_SLOTS)
        col = pl.multiple_of((step // 2) * 512, 512)
        row = pl.multiple_of(lax.rem(step, 2) * 3072, 3072)
        return pltpu.make_async_copy(w_up.at[pl.ds(row, 3072), pl.ds(col, 512)], wbuf.at[slot], wsem.at[slot])

    def fetch_down(step):
        slot = lax.rem(step + UP_STEPS, W_SLOTS)
        col = pl.multiple_of(step * 512, 512)
        return pltpu.make_async_copy(w_down.at[:, pl.ds(col, 512)], wbuf.at[slot], wsem.at[slot])

    head0 = core * 24 + a * 12 + b * 6
    wo_copy = pltpu.make_async_copy(w_out.at[pl.ds(pl.multiple_of(head0 * HD, HD), 6 * HD)], wobuf, wosem)
    my_copy = pltpu.make_async_copy(o_hbm.at[pl.ds(core * 24, 24)], mine, mysem)

    my_copy.start()
    enter([partner, n1, n2])

    def remote(src, dst, send, recv, peer):
        return pltpu.make_async_remote_copy(src_ref=src, dst_ref=dst, send_sem=send, recv_sem=recv,
                                            device_id=peer, device_id_type=MESH)

    o_send0 = remote(o_hbm.at[pl.ds((1 - core) * 24, 24)], orecv0, osend.at[0], orecv.at[0], partner)
    m_send0 = remote(ml_in, mlr.at[0], msend.at[0], mrecv.at[0], partner)
    m_send0.start()
    o_send0.start()
    for s in range(W_SLOTS):
        fetch_up(s).start()

    def up_block(n, carry):
        fetch_up(2 * n).wait()
        s0 = lax.rem(2 * n, W_SLOTS)
        acc = jnp.dot(normed[:, :3072], wbuf[s0], preferred_element_type=F32)
        fetch_up(2 * n + 1).wait()
        acc += jnp.dot(normed[:, 3072:], wbuf[s0 + 1], preferred_element_type=F32)
        for half in range(2):
            nxt = 2 * n + half + W_SLOTS

            @pl.when(nxt < UP_STEPS)
            def _():
                fetch_up(nxt).start()

            @pl.when(nxt >= UP_STEPS)
            def _():
                fetch_down(nxt - UP_STEPS).start()

        act[:, pl.ds(pl.multiple_of(n * 512, 512), 512)] = (
            0.5 * acc * (1.0 + lax.erf(acc * (2.0 ** -0.5)))).astype(BF16)
        return carry

    def down_block(n, carry):
        fetch_down(n).wait()
        acc = jnp.dot(act[...], wbuf[lax.rem(n + UP_STEPS, W_SLOTS)], preferred_element_type=F32)

        @pl.when(n + W_SLOTS < DOWN_STEPS)
        def _():
            fetch_down(n + W_SLOTS).start()

        for t in range(4):
            part[n * 4 + t] = acc[:, t * HD:(t + 1) * HD]
        return carry

    lanes = lax.broadcasted_iota(jnp.int32, (ROWS, HD), 1)

    def merge(stats, theirs, dst, dst0, recv, n):
        top = jnp.maximum(stats, theirs)
        w1 = jnp.exp(stats - top)
        w2 = jnp.exp(theirs - top)
        for h in range(n):
            dst[dst0 + h] = dst[dst0 + h] * w1[:, h:h + 1] + recv[h] * w2[:, h:h + 1]
        total = stats * pltpu.roll(w1, 64, 1) + theirs * pltpu.roll(w2, 64, 1)
        return jnp.where(lanes < 64, top, total)

    def shift(v, by):
        return pltpu.roll(v, lax.rem(HD - by, HD), 1)

    lax.fori_loop(0, 2, up_block, 0)

    my_copy.wait()
    m_send0.wait()
    o_send0.wait()
    ml0[0] = merge(shift(ml_in[...], core * 24), shift(mlr[0], core * 24), mine, 0, orecv0, 24)
    o_send1 = remote(mine.at[pl.ds((1 - a) * 12, 12)], orecv1, osend.at[1], orecv.at[1], n1)
    m_send1 = remote(ml0.at[0], mlr.at[1], msend.at[1], mrecv.at[1], n1)
    m_send1.start()
    o_send1.start()
    wo_copy.start()

    lax.fori_loop(2, 6, up_block, 0)
    lax.fori_loop(0, 4, down_block, 0)

    m_send1.wait()
    o_send1.wait()
    ml0[1] = merge(shift(ml0[0], a * 12), shift(mlr[1], a * 12), mine, a * 12, orecv1, 12)
    o_send2 = remote(mine.at[pl.ds(a * 12 + (1 - b) * 6, 6)], orecv2, osend.at[2], orecv.at[2], n2)
    m_send2 = remote(ml0.at[1], mlr.at[2], msend.at[2], mrecv.at[2], n2)
    m_send2.start()
    o_send2.start()

    lax.fori_loop(4, DOWN_STEPS, down_block, 0)

    m_send2.wait()
    o_send2.wait()
    mine0 = a * 12 + b * 6
    stats = merge(shift(ml0[1], b * 6), shift(mlr[2], b * 6), mine, mine0, orecv2, 6)
    for h in range(6):
        ctx[:, h * HD:(h + 1) * HD] = (mine[mine0 + h] / stats[:, 64 + h:65 + h]).astype(BF16)
    wo_copy.wait()

    half, quarter, eighth = CT // 2, CT // 4, CT // 8

    def p_send0(k):
        return remote(part.at[pl.ds(k * CT + (1 - core) * half, half)], precv0.at[k], psend.at[0, k], precv.at[0, k], partner)

    def p_send1(k):
        return remote(part.at[pl.ds(k * CT + core * half + (1 - a) * quarter, quarter)], precv1.at[k],
                      psend.at[1, k], precv.at[1, k], n1)

    def p_send2(k):
        return remote(part.at[pl.ds(k * CT + core * half + a * quarter + (1 - b) * eighth, eighth)], precv2.at[k],
                      psend.at[2, k], precv.at[2, k], n2)

    def spread(k, start, count, level, peer):
        where = gath.at[pl.ds(k * CT + start, count)]
        return remote(where, where, gsend.at[level, k], grecv.at[level, k], peer)

    def g_send2(k):
        return spread(k, core * half + a * quarter + b * eighth, eighth, 0, n2)

    def g_send1(k):
        return spread(k, core * half + a * quarter, quarter, 1, n1)

    def g_send0(k):
        return spread(k, core * half, half, 2, partner)

    def stage(s, k):
        if s == 0:
            def project(n, carry):
                t0 = k * CT + n * 4
                acc = jnp.dot(ctx[...], wobuf[:, pl.ds(pl.multiple_of(t0 * HD, 512), 512)], preferred_element_type=F32)
                for t in range(4):
                    part[t0 + t] += acc[:, t * HD:(t + 1) * HD]
                return carry

            lax.fori_loop(0, CT // 4, project, 0)
            p_send0(k).start()
        elif s == 1:
            p_send0(k).wait()
            base = k * CT + core * half
            part[pl.ds(base, half)] = part[pl.ds(base, half)] + precv0[k]
            p_send1(k).start()
        elif s == 2:
            p_send1(k).wait()
            base = k * CT + core * half + a * quarter
            part[pl.ds(base, quarter)] = part[pl.ds(base, quarter)] + precv1[k]
            p_send2(k).start()
        elif s == 3:
            p_send2(k).wait()
            base = k * CT + core * half + a * quarter + b * eighth
            for t in range(eighth):
                col = pl.multiple_of((base + t) * HD, HD)
                total = hid[:, pl.ds(col, HD)].astype(F32) + (part[base + t] + precv2[k, t])
                gath[base + t] = total.astype(BF16).astype(F32)
            g_send2(k).start()
        elif s == 4:
            g_send2(k).wait()
            g_send1(k).start()
        elif s == 5:
            g_send1(k).wait()
            g_send0(k).start()
        else:
            g_send0(k).wait()
            for t in range(CT):
                col = (k * CT + t) * HD
                out[:, col:col + HD] = gath[k * CT + t].astype(BF16)

    for wave in range(NK + 6):
        for k in range(NK):
            if 0 <= wave - k < 7:
                stage(wave - k, k)


def tail_call(normed, hidden, ml, o, w_up, w_down, w_out):
    vm = pl.BlockSpec(memory_space=pltpu.VMEM)
    anyspace = pl.BlockSpec(memory_space=pl.ANY)
    dma = pltpu.SemaphoreType.DMA
    return pl.pallas_call(
        tail_kernel,
        out_shape=jax.ShapeDtypeStruct((ROWS, D), BF16),
        in_specs=[vm, vm, vm, anyspace, anyspace, anyspace, anyspace],
        out_specs=vm,
        scratch_shapes=[
            pltpu.VMEM((W_SLOTS, 3072, 512), BF16),
            pltpu.VMEM((6 * HD, D), BF16),
            pltpu.VMEM((ROWS, FF), BF16),
            pltpu.VMEM((NH, ROWS, HD), F32),
            pltpu.VMEM((24, ROWS, HD), F32),
            pltpu.VMEM((24, ROWS, HD), F32),
            pltpu.VMEM((12, ROWS, HD), F32),
            pltpu.VMEM((6, ROWS, HD), F32),
            pltpu.VMEM((2, ROWS, HD), F32),
            pltpu.VMEM((3, ROWS, HD), F32),
            pltpu.VMEM((NK, CT // 2, ROWS, HD), F32),
            pltpu.VMEM((NK, CT // 4, ROWS, HD), F32),
            pltpu.VMEM((NK, CT // 8, ROWS, HD), F32),
            pltpu.VMEM((NH, ROWS, HD), F32),
            pltpu.VMEM((ROWS, 6 * HD), BF16),
            dma((W_SLOTS,)), dma, dma, dma((3,)), dma((3,)), dma((3,)), dma((3,)),
            dma((3, NK)), dma((3, NK)), dma((3, NK)), dma((3, NK)),
        ],
        compiler_params=pltpu.CompilerParams(collective_id=1, has_side_effects=True, vmem_limit_bytes=VMEM_LIMIT),
        cost_estimate=pl.CostEstimate(flops=4 * ROWS * D * FF, bytes_accessed=4 * D * FF, transcendentals=0),
        name='tail',
    )(normed, hidden, ml, o, w_up, w_down, w_out)


def device_step(hidden, ln_gamma, ln_beta, w_qkv, w_out, w_up, w_down, k_cache, v_cache, positions):
    cos, sin = rotary_tables(positions)
    local_pos = positions - lax.axis_index('sp') * SEQ
    qkv, normed = qkv_call(hidden, ln_gamma[None, :], ln_beta[None, :], cos, sin, w_qkv)
    o, ml, k_next, v_next = attn_call(local_pos, qkv, k_cache, v_cache)
    out = tail_call(normed, hidden, ml, o, w_up, w_down, w_out)
    return out, k_next, v_next


def solution(mesh):
    cache_spec = P('dp', 'sp', None)
    in_specs = (P('dp', None), P(None), P(None), P(None, None), P(None, None), P(None, 'sp'), P('sp', None), cache_spec, cache_spec, P('dp'))
    out_specs = (P('dp', None), cache_spec, cache_spec)
    return jax.shard_map(device_step, mesh=mesh, in_specs=in_specs, out_specs=out_specs, check_vma=False)
```

time: 349 us -> 140 us (0.40)
  Pallas kernels: 0 us -> 134 us
  waiting for transfers between devices: 121 us -> 0 us
  matrix products: 106 us -> 0 us
  other arithmetic: 77.6 us -> 2.4 us
  local copies, waits for them, and re-layouts: 29.8 us -> 2.69 us
  between operations: 14.3 us -> 0.67 us
    pallas_call x0 -> x3, Pallas kernels: none -> 134 us  [the longest x1 74.4 us: tail_call(): pl.pallas_call(tail_kernel, out_shape=jax.ShapeDtypeStruct((ROWS, D), BF1...]
    dot_general x5 -> x0, matrix products: 106 us -> none  [the longest x1 29.1 us: device_step(): mlp_part = jnp.dot(activated, w_down, preferred_element_type=jnp.float32)]
    all_gather x1 -> x0, waiting for transfers between devices: 100 us -> none  [device_step(): all_stats = lax.all_gather(block_stats, 'sp')]
    reduce_sum x5 -> x0, other arithmetic: 39 us -> none  [the longest x1 25.8 us: combine_stats(): total_ctx = jnp.sum(all_stats[..., :head_dim] * scale_w[..., None], axis=0)]
    select_n x1 -> x0, other arithmetic: 23.3 us -> none  [device_step(): v_next = jnp.where(write_mask, v_new[:, None, :], v_cache)]
    psum x1 -> x0, waiting for transfers between devices: 21.2 us -> none  [device_step(): mlp_out = lax.psum(mlp_part, 'sp')]
    unnamed x9 -> x1, local copies, waits for them, and re-layouts: 13.5 us -> 2.69 us
    concatenate x3 -> x0, other arithmetic: 7.85 us -> none  [the longest x1 7.65 us: local_stats(): jnp.concatenate([block_ctx, block_max[..., None], block_sum[..., None]],...]
  transfers between devices with their start and end apart: 2 -> 0, of which waited for: 2 -> 0; matrix products, arithmetic and copies ran while one was open for 20% -> 0% of each run, Pallas kernels for 0% -> 0%
where the time goes in v1:
time: 140 us; the launch traced here: 139 us
  Pallas kernels  134 us (96%)
  local copies, waits for them, and re-layouts  2.69 us (2%)
  other arithmetic  2.4 us (2%)
    pallas_call x1, Pallas kernels, tail_call(): pl.pallas_call(tail_kernel, out_shape=jax.ShapeDtypeStruct((ROWS, D), BF1...  74.4 us
    pallas_call x1, Pallas kernels, attn_call(): pl.pallas_call(attn_kernel, out_shape=(jax.ShapeDtypeStruct((NH, ROWS, HD...  40.1 us
    pallas_call x1, Pallas kernels, qkv_call(): pl.pallas_call(qkv_kernel, out_shape=(jax.ShapeDtypeStruct((NH + 2, ROWS,...  19.2 us

profile of v1, /device:TPU:0, one launch (start us, length us, event | category | flops | bytes accessed | tf_op | source)
XLA Modules:
  0.0 139.4 jit_solution(13312378985575285890)
XLA Ops:
  0.6 1.3 broadcast_subtract_fusion
  2.0 0.3 fusion
  2.3 0.8 pad_maximum_fusion
  3.0 19.2 %qkv.1 = (f32[50,128,128]{2,1,0:T(8,128)}, bf16[128,6144]{1,0:T(8,128)(2,1)}) custom-call(bf16[128,6144]{1,0:T(8,128)(2,1)} %hid.3, f32[1,6144]{1,0:T(1,128)} %bitcast.2, f32[1,6144]{1,0:T(1,128)} %bitcast.3, f32[128,128]{1,0:T(8,128)} %get-tuple-element.20.cos, f32[128,128]{1,0:T(8,128)} %get-tuple-element.21.sin, bf16[6144,6400]{1,0:T(8,128)(2,1)} %w.1), custom_call_target="tpu_custom_call" | custom-call | flops 5033164800 | bytes 39321600 | tf_op jit(solution)/shard_map/qkv/pallas_call | solution.py:126
  22.3 40.1 %attn.1 = (f32[48,128,128]{2,1,0:T(8,128)}, f32[128,128]{1,0:T(8,128)}, bf16[128,512,128]{2,1,0:T(8,128)(2,1)}, bf16[128,512,128]{2,1,0:T(8,128)(2,1)}) custom-call(s32[128]{0:T(128)} %get-tuple-element.18.lp_ref, f32[50,128,128]{2,1,0:T(8,128)} %get-tuple-element.10.qkv, bf16[128,512,128]{2,1,0:T(8,128)(2,1)} %kc.1, bf16[128,512,128]{2,1,0:T(8,128)(2,1)} %vc.1), custom_call_target="tpu_custom_call" | custom-call | flops 1610612736 | bytes 67108864 | tf_op jit(solution)/shard_map/attn/pallas_call | solution.py:225
  62.4 74.4 %tail.1 = bf16[128,6144]{1,0:T(8,128)(2,1)} custom-call(bf16[128,6144]{1,0:T(8,128)(2,1)} %get-tuple-element.9.normed, bf16[128,6144]{1,0:T(8,128)(2,1)} %hid.3, f32[128,128]{1,0:T(8,128)} %get-tuple-element.11.ml_in, f32[48,128,128]{2,1,0:T(8,128)} %get-tuple-element.12.o_hbm, bf16[6144,3072]{1,0:T(8,128)(2,1)} %w_up.1, bf16[3072,6144]{1,0:T(8,128)(2,1)} %w_down.1, ...), custom_call_target="tpu_custom_call" | custom-call | flops 9663676416 | bytes 75497472 | tf_op jit(solution)/shard_map/tail/pallas_call | solution.py:452
  136.7 2.7 %copy.14 = bf16[128,6144]{1,0:T(8,128)(2,1)} copy(bf16[128,6144]{1,0:T(8,128)(2,1)} %tail.1) | data formatting | bytes 3145728
  (1 shorter events, 0.0 us)

commit v2 on v1

v2 whole, which is shorter than its diff:
```python
import functools

import jax
import jax.numpy as jnp
from jax import lax
from jax.experimental import pallas as pl
from jax.experimental.pallas import tpu as pltpu
from jax.sharding import PartitionSpec as P

LN_EPS = 1e-5
ROPE_BASE = 10000.0
NEG_FILL = -1e30
SCALE2 = 128 ** -0.5 * 1.4426950408889634
MESH = pl.DeviceIdType.MESH
VMEM_LIMIT = 67_000_000

ROWS = 128
D = 6144
HD = 128
NH = 48
SEQ = 512
FF = 3072
F32 = jnp.float32
BF16 = jnp.bfloat16


def rotary_tables(positions):
    inv_freq = 1.0 / (ROPE_BASE ** (jnp.arange(0, HD, 2, dtype=F32) / HD))
    angles = positions.astype(F32)[:, None] * inv_freq[None, :]
    cos_half = jnp.cos(angles)
    sin_half = jnp.sin(angles)
    return jnp.concatenate([cos_half, cos_half], axis=-1), jnp.concatenate([-sin_half, sin_half], axis=-1)


def place():
    sp = lax.axis_index('sp')
    core = lax.rem(sp, 2)
    x = lax.rem(sp // 2, 2)
    y = sp // 4
    return y, x, core


def device(y, x, core):
    return {'sp': (y * 2 + x) * 2 + core}


def enter(peers):
    barrier = pltpu.get_barrier_semaphore()
    for peer in peers:
        pl.semaphore_signal(barrier, inc=1, device_id=peer, device_id_type=MESH)
    pl.semaphore_wait(barrier, len(peers))


Q_STEPS = 12
Q_SLOTS = 6
Q_HALF = NH // 2


def qkv_kernel(hid, gam, bet, cos, sin, w, qkv, normed, wbuf, wkv, mine, wsem, kvsem, lsem, ssem, rsem):
    y, x, core = place()
    partner = device(y, x, 1 - core)

    def fetch(j):
        col = pl.multiple_of(core * (Q_HALF * HD) + j * 256, 256)
        slot = lax.rem(j, Q_SLOTS)
        return pltpu.make_async_copy(w.at[:, pl.ds(col, 256)], wbuf.at[slot], wsem.at[slot])

    kv_copy = pltpu.make_async_copy(w.at[:, pl.ds(pl.multiple_of((NH + core) * HD, HD), HD)], wkv, kvsem)
    kv_copy.start()
    for j in range(Q_SLOTS):
        fetch(j).start()
    enter([partner])

    def norm_rows(i, carry):
        rows = pl.ds(pl.multiple_of(i * 16, 16), 16)
        v = hid[rows, :].astype(F32)
        mean = jnp.sum(v, axis=-1, keepdims=True) * (1.0 / D)
        cen = v - mean
        var = jnp.sum(cen * cen, axis=-1, keepdims=True) * (1.0 / D)
        normed[rows, :] = (cen * lax.rsqrt(var + LN_EPS) * gam[...] + bet[...]).astype(BF16)
        return carry

    lax.fori_loop(0, ROWS // 16, norm_rows, 0)

    def remote(src, dst, count, sem):
        return pltpu.make_async_remote_copy(
            src_ref=mine.at[pl.ds(src, count)], dst_ref=qkv.at[pl.ds(dst, count)],
            send_sem=ssem.at[sem], recv_sem=rsem.at[sem], device_id=partner, device_id_type=MESH)

    def local(src, dst, count, sem):
        return pltpu.make_async_copy(mine.at[pl.ds(src, count)], qkv.at[pl.ds(dst, count)], lsem.at[sem])

    def pair(j):
        return 2 * j, core * Q_HALF + 2 * j, 2, j

    kv = (Q_HALF, NH + core, 1, Q_STEPS)

    def rotate(v):
        return (v * cos[...] + pltpu.roll(v, 64, 1) * sin[...]).astype(BF16).astype(F32)

    kv_copy.wait()
    v = jnp.dot(normed[...], wkv[...], preferred_element_type=F32).astype(BF16).astype(F32)
    mine[Q_HALF] = jnp.where(core == 0, rotate(v), v)
    remote(*kv).start()
    local(*kv).start()

    def block(j, carry):
        fetch(j).wait()
        acc = jnp.dot(normed[...], wbuf[lax.rem(j, Q_SLOTS)], preferred_element_type=F32)

        @pl.when(j + Q_SLOTS < Q_STEPS)
        def _():
            fetch(j + Q_SLOTS).start()

        for h in range(2):
            mine[2 * j + h] = rotate(acc[:, h * HD:(h + 1) * HD].astype(BF16).astype(F32))
        remote(*pair(j)).start()
        local(*pair(j)).start()
        return carry

    lax.fori_loop(0, Q_STEPS, block, 0)

    def drain(j, carry):
        local(*pair(j)).wait()
        remote(*pair(j)).wait()
        return carry

    lax.fori_loop(0, Q_STEPS, drain, 0)
    local(*kv).wait()
    remote(*kv).wait()


def qkv_call(hidden, gam, bet, cos, sin, w_qkv):
    vm = pl.BlockSpec(memory_space=pltpu.VMEM)
    anyspace = pl.BlockSpec(memory_space=pl.ANY)
    dma = pltpu.SemaphoreType.DMA
    return pl.pallas_call(
        qkv_kernel,
        out_shape=(jax.ShapeDtypeStruct((NH + 2, ROWS, HD), F32), jax.ShapeDtypeStruct((ROWS, D), BF16)),
        in_specs=[vm, vm, vm, vm, vm, anyspace],
        out_specs=(anyspace, vm),
        scratch_shapes=[
            pltpu.VMEM((Q_SLOTS, D, 256), BF16),
            pltpu.VMEM((D, HD), BF16),
            pltpu.VMEM((Q_HALF + 1, ROWS, HD), F32),
            dma((Q_SLOTS,)), dma, dma((Q_STEPS + 1,)), dma((Q_STEPS + 1,)), dma((Q_STEPS + 1,)),
        ],
        compiler_params=pltpu.CompilerParams(collective_id=0, has_side_effects=True, vmem_limit_bytes=VMEM_LIMIT),
        cost_estimate=pl.CostEstimate(flops=2 * ROWS * D * 3200, bytes_accessed=D * 6400, transcendentals=0),
        name='qkv',
    )(hidden, gam, bet, cos, sin, w_qkv)


A_ROWS = 8
A_STEPS = ROWS // A_ROWS
A_SLOTS = 8
A_AHEAD = 4


def attn_kernel(lp_ref, qkv, kc, vc, o, ml, kn, vn, kbuf, vbuf, sbuf, ebuf, isem, osem):
    i = pl.program_id(0)

    def fetch(step):
        slot = lax.rem(step, A_SLOTS)
        rows = pl.ds(step * A_ROWS, A_ROWS)
        return (pltpu.make_async_copy(kc.at[rows], kbuf.at[slot], isem.at[0, slot]),
                pltpu.make_async_copy(vc.at[rows], vbuf.at[slot], isem.at[1, slot]))

    def flush(step):
        slot = lax.rem(step, A_SLOTS)
        rows = pl.ds(step * A_ROWS, A_ROWS)
        return (pltpu.make_async_copy(kbuf.at[slot], kn.at[rows], osem.at[0, slot]),
                pltpu.make_async_copy(vbuf.at[slot], vn.at[rows], osem.at[1, slot]))

    @pl.when(i == 0)
    def _():
        for s in range(A_AHEAD):
            for c in fetch(s):
                c.start()

    @pl.when(i >= A_AHEAD)
    def _():
        for c in flush(i - A_AHEAD):
            c.wait()

    @pl.when(i + A_AHEAD < A_STEPS)
    def _():
        for c in fetch(i + A_AHEAD):
            c.start()

    for c in fetch(i):
        c.wait()
    slot = lax.rem(i, A_SLOTS)

    for r in range(A_ROWS):
        lp = lp_ref[i * A_ROWS + r]
        base = pl.multiple_of((jnp.clip(lp, 0, SEQ - 1) // 16) * 16, 16)
        hit = base + lax.broadcasted_iota(jnp.int32, (16, HD), 0) == lp
        for buf, src in ((kbuf, NH), (vbuf, NH + 1)):
            new = jnp.broadcast_to(qkv[src, r:r + 1, :], (16, HD))
            old = buf[slot, r, pl.ds(base, 16), :].astype(F32)
            buf[slot, r, pl.ds(base, 16), :] = jnp.where(hit, new, old).astype(BF16)

    for r in range(A_ROWS):
        q = qkv[0:NH, r, :].astype(BF16)
        sbuf[r] = lax.dot_general(q, kbuf[slot, r], (((1,), (1,)), ((), ())), preferred_element_type=F32)
    lane = lax.broadcasted_iota(jnp.int32, (NH, HD), 1)
    mcol = jnp.zeros((NH, HD), F32)
    lcol = jnp.zeros((NH, HD), F32)
    for r in range(A_ROWS):
        valid = lax.broadcasted_iota(jnp.int32, (NH, SEQ), 1) <= lp_ref[i * A_ROWS + r]
        s = jnp.where(valid, sbuf[r], -jnp.inf)
        m = jnp.max(s, axis=-1, keepdims=True)
        m = jnp.where(m == -jnp.inf, NEG_FILL, m)
        e = jnp.exp2((s - m) * SCALE2)
        l = jnp.sum(e, axis=-1, keepdims=True)
        ebuf[r] = e.astype(BF16)
        mcol = jnp.where(lane == r, m * SCALE2, mcol)
        lcol = jnp.where(lane == r, l, lcol)
    for r in range(A_ROWS):
        o[:, r, :] = jnp.dot(ebuf[r], vbuf[slot, r], preferred_element_type=F32)
    pad = jnp.zeros((16, HD), F32)
    ml[...] = jnp.transpose(jnp.concatenate([mcol, pad, lcol, pad], axis=0))[:A_ROWS]

    for c in flush(i):
        c.start()

    @pl.when(i == A_STEPS - 1)
    def _():
        for step in range(A_STEPS - A_AHEAD, A_STEPS):
            for c in flush(step):
                c.wait()


def attn_call(local_pos, qkv, k_cache, v_cache):
    anyspace = pl.BlockSpec(memory_space=pl.ANY)
    cache = jax.ShapeDtypeStruct((ROWS, SEQ, HD), BF16)
    return pl.pallas_call(
        attn_kernel,
        out_shape=(jax.ShapeDtypeStruct((NH, ROWS, HD), F32), jax.ShapeDtypeStruct((ROWS, HD), F32), cache, cache),
        grid_spec=pltpu.PrefetchScalarGridSpec(
            num_scalar_prefetch=1,
            grid=(A_STEPS,),
            in_specs=[pl.BlockSpec((NH + 2, A_ROWS, HD), lambda i, p: (0, i, 0)), anyspace, anyspace],
            out_specs=(pl.BlockSpec((NH, A_ROWS, HD), lambda i, p: (0, i, 0)), pl.BlockSpec((A_ROWS, HD), lambda i, p: (i, 0)),
                       anyspace, anyspace),
            scratch_shapes=[
                pltpu.VMEM((A_SLOTS, A_ROWS, SEQ, HD), BF16),
                pltpu.VMEM((A_SLOTS, A_ROWS, SEQ, HD), BF16),
                pltpu.VMEM((A_ROWS, NH, SEQ), F32),
                pltpu.VMEM((A_ROWS, NH, SEQ), BF16),
                pltpu.SemaphoreType.DMA((2, A_SLOTS)),
                pltpu.SemaphoreType.DMA((2, A_SLOTS)),
            ]),
        compiler_params=pltpu.CompilerParams(vmem_limit_bytes=VMEM_LIMIT, dimension_semantics=('arbitrary',)),
        cost_estimate=pl.CostEstimate(flops=4 * ROWS * NH * SEQ * HD, bytes_accessed=8 * ROWS * SEQ * HD, transcendentals=0),
        name='attn',
    )(local_pos, qkv, k_cache, v_cache)


W_SLOTS = 8
UP_STEPS = 12
DOWN_STEPS = 12
NR = 2
RT = NH // NR
NK = 3
CT = NH // NK
DOWN_PER = DOWN_STEPS // NK
OWN = NH // 8
LEVELS = 3


def tail_kernel(normed_hbm, hid_hbm, ml_in, o_hbm, w_up, w_down, w_out, out,
                normed, hid, wbuf, wobuf, act, part, mine, orecv0, orecv1, orecv2, stats, mlr, wts,
                precv0, precv1, precv2, gath, ctx, outbuf,
                insem, wsem, wosem, mysem, osend, orecv, msend, mrecv, psend, precv, gsend, grecv, outsem):
    y, x, core = place()
    first = 1 - core
    partner = device(y, x, 1 - core)
    x_peer = device(y, 1 - x, core)['sp']
    y_peer = device(1 - y, x, core)['sp']
    n1 = {'sp': x_peer * first + y_peer * core}
    n2 = {'sp': y_peer * first + x_peer * core}
    a = x * first + y * core
    b = y * first + x * core
    peers = (partner, n1, n2)

    def own(tiles, level):
        start = core * (tiles // 2)
        if level >= 1:
            start += a * (tiles // 4)
        if level >= 2:
            start += b * (tiles // 8)
        return start

    def other(tiles, level):
        start = 0 if level == 0 else own(tiles, level - 1)
        return start + (1 - (core, a, b)[level]) * (tiles // (2, 4, 8)[level])

    def remote(src, dst, send, recv, peer):
        return pltpu.make_async_remote_copy(src_ref=src, dst_ref=dst, send_sem=send, recv_sem=recv,
                                            device_id=peer, device_id_type=MESH)

    def fetch_up(step):
        slot = lax.rem(step, W_SLOTS)
        col = pl.multiple_of((step // 2) * 512, 512)
        row = pl.multiple_of(lax.rem(step, 2) * 3072, 3072)
        return pltpu.make_async_copy(w_up.at[pl.ds(row, 3072), pl.ds(col, 512)], wbuf.at[slot], wsem.at[slot])

    def fetch_down(step):
        slot = lax.rem(step + UP_STEPS, W_SLOTS)
        col = pl.multiple_of(step * 512, 512)
        return pltpu.make_async_copy(w_down.at[:, pl.ds(col, 512)], wbuf.at[slot], wsem.at[slot])

    normed_copy = pltpu.make_async_copy(normed_hbm, normed, insem.at[0])
    hid_copy = pltpu.make_async_copy(hid_hbm, hid, insem.at[1])

    def my_copy(k):
        return pltpu.make_async_copy(o_hbm.at[pl.ds(k * RT + own(RT, 0), RT // 2)], mine.at[k], mysem.at[k])

    def wo_copy(k):
        rows = pl.ds(pl.multiple_of((k * RT + own(RT, 2)) * HD, HD), RT // 8 * HD)
        return pltpu.make_async_copy(w_out.at[rows], wobuf.at[pl.ds(k * (RT // 8 * HD), RT // 8 * HD)], wosem.at[k])

    def out_copy(k):
        cols = pl.ds(k * CT * HD, CT * HD)
        return pltpu.make_async_copy(outbuf.at[:, cols], out.at[:, cols], outsem.at[k])

    o_to = (orecv0, orecv1, orecv2)

    def o_send(level, k):
        if level == 0:
            src = o_hbm.at[pl.ds(k * RT + other(RT, 0), RT // 2)]
        else:
            src = mine.at[k, pl.ds(other(RT, level) - own(RT, 0), RT // (2, 4, 8)[level])]
        return remote(src, o_to[level].at[k], osend.at[level, k], orecv.at[level, k], peers[level])

    def m_send(level):
        src = ml_in if level == 0 else stats.at[level - 1]
        return remote(src, mlr.at[level], msend.at[level], mrecv.at[level], peers[level])

    lanes = lax.broadcasted_iota(jnp.int32, (ROWS, HD), 1)

    def merge_stats(level):
        m_send(level).wait()
        ours = ml_in[...] if level == 0 else stats[level - 1]
        theirs = mlr[level]
        top = jnp.maximum(ours, theirs)
        w1 = jnp.exp2(ours - top)
        w2 = jnp.exp2(theirs - top)
        total = ours * pltpu.roll(w1, 64, 1) + theirs * pltpu.roll(w2, 64, 1)
        wts[level, 0] = w1
        wts[level, 1] = w2
        stats[level] = jnp.where(lanes < 64, top, total)

    def shift(v, by):
        return pltpu.roll(v, lax.rem(HD - by, HD), 1)

    def merge_heads(level, k):
        if level == 0:
            my_copy(k).wait()
        o_send(level, k).wait()
        first_head = k * RT + own(RT, level)
        w1 = shift(wts[level, 0], first_head)
        w2 = shift(wts[level, 1], first_head)
        base = own(RT, level) - own(RT, 0)
        for h in range(RT // (2, 4, 8)[level]):
            mine[k, base + h] = mine[k, base + h] * w1[:, h:h + 1] + o_to[level][k, h] * w2[:, h:h + 1]
        if level < 2:
            if k == 0:
                m_send(level + 1).start()
            o_send(level + 1, k).start()
        else:
            l = shift(stats[2], first_head)
            for h in range(RT // 8):
                col = (k * (RT // 8) + h) * HD
                ctx[:, col:col + HD] = (mine[k, base + h] / l[:, 64 + h:65 + h]).astype(BF16)

    def up_block(n, carry):
        fetch_up(2 * n).wait()
        s0 = lax.rem(2 * n, W_SLOTS)
        acc = jnp.dot(normed[:, :3072], wbuf[s0], preferred_element_type=F32)
        fetch_up(2 * n + 1).wait()
        acc += jnp.dot(normed[:, 3072:], wbuf[s0 + 1], preferred_element_type=F32)
        for half in range(2):
            nxt = 2 * n + half + W_SLOTS

            @pl.when(nxt < UP_STEPS)
            def _():
                fetch_up(nxt).start()

            @pl.when(nxt >= UP_STEPS)
            def _():
                fetch_down(nxt - UP_STEPS).start()

        act[:, pl.ds(pl.multiple_of(n * 512, 512), 512)] = (
            0.5 * acc * (1.0 + lax.erf(acc * (2.0 ** -0.5)))).astype(BF16)
        return carry

    def down_block(n, carry):
        fetch_down(n).wait()
        acc = jnp.dot(act[...], wbuf[lax.rem(n + UP_STEPS, W_SLOTS)], preferred_element_type=F32)

        @pl.when(n + W_SLOTS < DOWN_STEPS)
        def _():
            fetch_down(n + W_SLOTS).start()

        for t in range(4):
            part[n * 4 + t] = acc[:, t * HD:(t + 1) * HD]
        return carry

    def up(lo, hi):
        lax.fori_loop(lo, hi, up_block, 0)

    def down(lo, hi):
        lax.fori_loop(lo, hi, down_block, 0)

    p_to = (precv0, precv1, precv2)

    def p_send(level, k):
        src = part.at[pl.ds(k * CT + other(CT, level), CT // (2, 4, 8)[level])]
        return remote(src, p_to[level].at[k], psend.at[level, k], precv.at[level, k], peers[level])

    def g_send(level, k):
        where = gath.at[pl.ds(k * CT + own(CT, level), CT // (2, 4, 8)[level])]
        return remote(where, where, gsend.at[level, k], grecv.at[level, k], peers[level])

    def project(k):
        def tiles(n, carry):
            t0 = k * CT + n * 4
            acc = jnp.dot(ctx[...], wobuf[:, pl.ds(pl.multiple_of(t0 * HD, 512), 512)], preferred_element_type=F32)
            for t in range(4):
                part[t0 + t] += acc[:, t * HD:(t + 1) * HD]
            return carry

        lax.fori_loop(0, CT // 4, tiles, 0)
        p_send(0, k).start()

    def reduce(level, k):
        p_send(level, k).wait()
        base, count = k * CT + own(CT, level), CT // (2, 4, 8)[level]
        if level < 2:
            part[pl.ds(base, count)] = part[pl.ds(base, count)] + p_to[level][k]
            p_send(level + 1, k).start()
        else:
            for t in range(count):
                col = pl.multiple_of((base + t) * HD, HD)
                total = hid[:, pl.ds(col, HD)].astype(F32) + (part[base + t] + p_to[2][k, t])
                gath[base + t] = total.astype(BF16).astype(F32)
            g_send(2, k).start()

    def gather(level, k):
        g_send(level, k).wait()
        if level > 0:
            g_send(level - 1, k).start()
        else:
            for t in range(CT):
                col = (k * CT + t) * HD
                outbuf[:, col:col + HD] = gath[k * CT + t].astype(BF16)
            out_copy(k).start()

    normed_copy.start()
    for k in range(NR):
        my_copy(k).start()
    enter(peers)
    m_send(0).start()
    for k in range(NR):
        o_send(0, k).start()
    for s in range(W_SLOTS):
        fetch_up(s).start()
    normed_copy.wait()

    up(0, 1)
    merge_stats(0)
    merge_heads(0, 0)
    merge_heads(0, 1)
    up(1, 4)
    merge_stats(1)
    merge_heads(1, 0)
    for k in range(NR):
        wo_copy(k).start()
    hid_copy.start()
    up(4, 6)
    down(0, 1)
    merge_heads(1, 1)
    down(1, 4)
    merge_stats(2)
    merge_heads(2, 0)
    down(4, 6)
    merge_heads(2, 1)
    for k in range(NR):
        wo_copy(k).wait()
    hid_copy.wait()
    project(0)
    down(6, 8)
    project(1)
    reduce(0, 0)
    down(8, 12)
    project(2)
    reduce(0, 1)
    reduce(0, 2)
    for wave in range(1, NK + 5):
        for k in range(NK):
            s = wave - k
            if 1 <= s <= 2:
                reduce(s, k)
            elif 3 <= s <= 5:
                gather(5 - s, k)
    for k in range(NK):
        out_copy(k).wait()


def tail_call(normed, hidden, ml, o, w_up, w_down, w_out):
    vm = pl.BlockSpec(memory_space=pltpu.VMEM)
    anyspace = pl.BlockSpec(memory_space=pl.ANY)
    dma = pltpu.SemaphoreType.DMA
    return pl.pallas_call(
        tail_kernel,
        out_shape=jax.ShapeDtypeStruct((ROWS, D), BF16),
        in_specs=[anyspace, anyspace, vm, anyspace, anyspace, anyspace, anyspace],
        out_specs=anyspace,
        scratch_shapes=[
            pltpu.VMEM((ROWS, D), BF16),
            pltpu.VMEM((ROWS, D), BF16),
            pltpu.VMEM((W_SLOTS, 3072, 512), BF16),
            pltpu.VMEM((OWN * HD, D), BF16),
            pltpu.VMEM((ROWS, FF), BF16),
            pltpu.VMEM((NH, ROWS, HD), F32),
            pltpu.VMEM((NR, RT // 2, ROWS, HD), F32),
            pltpu.VMEM((NR, RT // 2, ROWS, HD), F32),
            pltpu.VMEM((NR, RT // 4, ROWS, HD), F32),
            pltpu.VMEM((NR, RT // 8, ROWS, HD), F32),
            pltpu.VMEM((LEVELS, ROWS, HD), F32),
            pltpu.VMEM((LEVELS, ROWS, HD), F32),
            pltpu.VMEM((LEVELS, 2, ROWS, HD), F32),
            pltpu.VMEM((NK, CT // 2, ROWS, HD), F32),
            pltpu.VMEM((NK, CT // 4, ROWS, HD), F32),
            pltpu.VMEM((NK, CT // 8, ROWS, HD), F32),
            pltpu.VMEM((NH, ROWS, HD), F32),
            pltpu.VMEM((ROWS, OWN * HD), BF16),
            pltpu.VMEM((ROWS, D), BF16),
            dma((2,)), dma((W_SLOTS,)), dma((NR,)), dma((NR,)),
            dma((LEVELS, NR)), dma((LEVELS, NR)), dma((LEVELS,)), dma((LEVELS,)),
            dma((LEVELS, NK)), dma((LEVELS, NK)), dma((LEVELS, NK)), dma((LEVELS, NK)), dma((NK,)),
        ],
        compiler_params=pltpu.CompilerParams(collective_id=1, has_side_effects=True, vmem_limit_bytes=VMEM_LIMIT),
        cost_estimate=pl.CostEstimate(flops=4 * ROWS * D * FF, bytes_accessed=4 * D * FF, transcendentals=0),
        name='tail',
    )(normed, hidden, ml, o, w_up, w_down, w_out)


def device_step(hidden, ln_gamma, ln_beta, w_qkv, w_out, w_up, w_down, k_cache, v_cache, positions):
    cos, sin = rotary_tables(positions)
    local_pos = positions - lax.axis_index('sp') * SEQ
    qkv, normed = qkv_call(hidden, ln_gamma[None, :], ln_beta[None, :], cos, sin, w_qkv)
    o, ml, k_next, v_next = attn_call(local_pos, qkv, k_cache, v_cache)
    out = tail_call(normed, hidden, ml, o, w_up, w_down, w_out)
    return out, k_next, v_next


def solution(mesh):
    cache_spec = P('dp', 'sp', None)
    in_specs = (P('dp', None), P(None), P(None), P(None, None), P(None, None), P(None, 'sp'), P('sp', None), cache_spec, cache_spec, P('dp'))
    out_specs = (P('dp', None), cache_spec, cache_spec)
    return jax.shard_map(device_step, mesh=mesh, in_specs=in_specs, out_specs=out_specs, check_vma=False)
```

time: 140 us -> 123 us (0.88)
  Pallas kernels: 134 us -> 117 us
    pallas_call x1, Pallas kernels: 40.1 us -> 28.6 us  [attn_call(): pl.pallas_call(attn_kernel, out_shape=(jax.ShapeDtypeStruct((NH, ROWS, HD...]
    pallas_call x1, Pallas kernels: 74.4 us -> 68.5 us  [tail_call(): pl.pallas_call(tail_kernel, out_shape=jax.ShapeDtypeStruct((ROWS, D), BF1...]
where the time goes in v2:
time: 123 us
  Pallas kernels  117 us (95%)
  local copies, waits for them, and re-layouts  2.69 us (2%)
  other arithmetic  2.4 us (2%)
    pallas_call x1, Pallas kernels, tail_call(): pl.pallas_call(tail_kernel, out_shape=jax.ShapeDtypeStruct((ROWS, D), BF1...  68.5 us
    pallas_call x1, Pallas kernels, attn_call(): pl.pallas_call(attn_kernel, out_shape=(jax.ShapeDtypeStruct((NH, ROWS, HD...  28.6 us
    pallas_call x1, Pallas kernels, qkv_call(): pl.pallas_call(qkv_kernel, out_shape=(jax.ShapeDtypeStruct((NH + 2, ROWS,...  19.7 us
    unnamed x1, local copies, waits for them, and re-layouts  2.69 us

profile of v2, /device:TPU:0, one launch (start us, length us, event | category | flops | bytes accessed | tf_op | source)
XLA Modules:
  0.0 122.5 jit_solution(7487449175224753664)
XLA Ops:
  0.6 1.3 %broadcast_subtract_fusion = (s32[128]{0:T(128)}, f32[128]{0:T(128)S(1)}) fusion(s32[128]{0:T(128)} %param.19, s32[]{:T(128)S(6)} %mul.22), kind=kLoop, calls=%fused_computation.6 | loop fusion | flops 256 | bytes 1540 | tf_op jit(solution)/shard_map/sub | solution.py:554
  2.0 0.3 fusion
  2.3 0.8 pad_maximum_fusion
  3.0 19.7 %qkv.1 = (f32[50,128,128]{2,1,0:T(8,128)}, bf16[128,6144]{1,0:T(8,128)(2,1)}) custom-call(bf16[128,6144]{1,0:T(8,128)(2,1)} %hid_hbm.1, f32[1,6144]{1,0:T(1,128)} %bitcast.2, f32[1,6144]{1,0:T(1,128)} %bitcast.3, f32[128,128]{1,0:T(8,128)} %get-tuple-element.20.cos, f32[128,128]{1,0:T(8,128)} %get-tuple-element.21.sin, bf16[6144,6400]{1,0:T(8,128)(2,1)} %w.1), custom_call_target="tpu_custom_call" | custom-call | flops 5033164800 | bytes 39321600 | tf_op jit(solution)/shard_map/qkv/pallas_call | solution.py:137
  22.7 28.6 %attn.1 = (f32[48,128,128]{2,1,0:T(8,128)}, f32[128,128]{1,0:T(8,128)}, bf16[128,512,128]{2,1,0:T(8,128)(2,1)}, bf16[128,512,128]{2,1,0:T(8,128)(2,1)}) custom-call(s32[128]{0:T(128)} %get-tuple-element.18.lp_ref, f32[50,128,128]{2,1,0:T(8,128)} %get-tuple-element.10.qkv, bf16[128,512,128]{2,1,0:T(8,128)(2,1)} %kc.1, bf16[128,512,128]{2,1,0:T(8,128)(2,1)} %vc.1), custom_call_target="tpu_custom_call" | custom-call | flops 1610612736 | bytes 67108864 | tf_op jit(solution)/shard_map/attn/pallas_call | solution.py:238
  51.3 68.5 %tail.1 = bf16[128,6144]{1,0:T(8,128)(2,1)} custom-call(bf16[128,6144]{1,0:T(8,128)(2,1)} %get-tuple-element.9.normed_hbm, bf16[128,6144]{1,0:T(8,128)(2,1)} %hid_hbm.1, f32[128,128]{1,0:T(8,128)} %get-tuple-element.11.ml_in, f32[48,128,128]{2,1,0:T(8,128)} %get-tuple-element.12.o_hbm, bf16[6144,3072]{1,0:T(8,128)(2,1)} %w_up.1, bf16[3072,6144]{1,0:T(8,128)(2,1)} %w_down.1, ...), custom_call_target="tpu_custom_call" | custom-call | flops 9663676416 | bytes 75497472 | tf_op jit(solution)/shard_map/tail/pallas_call | solution.py:517
  119.8 2.7 %copy.14 = bf16[128,6144]{1,0:T(8,128)(2,1)} copy(bf16[128,6144]{1,0:T(8,128)(2,1)} %tail.1) | data formatting | bytes 3145728
  (1 shorter events, 0.0 us)

commit v3 on v2

v3 whole, which is shorter than its diff:
```python
import functools

import jax
import jax.numpy as jnp
from jax import lax
from jax.experimental import pallas as pl
from jax.experimental.pallas import tpu as pltpu
from jax.sharding import PartitionSpec as P

LN_EPS = 1e-5
ROPE_BASE = 10000.0
NEG_FILL = -1e30
SCALE2 = 128 ** -0.5 * 1.4426950408889634
MESH = pl.DeviceIdType.MESH
FRONT_LIMIT = 46_000_000
ATTN_LIMIT = 40_000_000
TAIL_LIMIT = 48_500_000

ROWS = 128
D = 6144
HD = 128
NH = 48
SEQ = 512
FF = 3072
F32 = jnp.float32
BF16 = jnp.bfloat16


def device(y, x, core):
    return {'sp': (y * 2 + x) * 2 + core}


class Place:
    def __init__(self):
        sp = lax.axis_index('sp')
        core = lax.rem(sp, 2)
        x = lax.rem(sp // 2, 2)
        y = sp // 4
        first = 1 - core
        x_peer = device(y, 1 - x, core)['sp']
        y_peer = device(1 - y, x, core)['sp']
        self.sides = (core, x * first + y * core, y * first + x * core)
        self.peers = (device(y, x, first), {'sp': x_peer * first + y_peer * core}, {'sp': y_peer * first + x_peer * core})

    def own(self, tiles, level):
        return sum(self.sides[n] * (tiles // (2, 4, 8)[n]) for n in range(level + 1))

    def other(self, tiles, level):
        start = self.own(tiles, level - 1) if level else 0
        return start + (1 - self.sides[level]) * (tiles // (2, 4, 8)[level])

    def remote(self, level, src, dst, send, recv):
        return pltpu.make_async_remote_copy(src_ref=src, dst_ref=dst, send_sem=send, recv_sem=recv,
                                            device_id=self.peers[level], device_id_type=MESH)

    def enter(self):
        barrier = pltpu.get_barrier_semaphore()
        for peer in self.peers:
            pl.semaphore_signal(barrier, inc=1, device_id=peer, device_id_type=MESH)
        pl.semaphore_wait(barrier, len(self.peers))


PART = (2, 4, 8)
LEVELS = 3


NQ = 3
QT = NH // NQ
U_SLOTS = 6
UP_STEPS = 12


def front_kernel(hid, gam, bet, pos, freq, w, w_up, qkv, act, normed, qbuf, wbuf, cos, sin, qsem, wsem, gsend, grecv):
    here = Place()

    def fetch_q(k):
        col = k * QT + here.own(QT, 2) if k < NQ else NH
        return pltpu.make_async_copy(w.at[:, pl.ds(pl.multiple_of(col * HD, 256), 256)], qbuf.at[k], qsem.at[k])

    def fetch_up(step):
        slot = lax.rem(step, U_SLOTS)
        col = pl.multiple_of((step // 2) * 512, 512)
        row = pl.multiple_of(lax.rem(step, 2) * 3072, 3072)
        return pltpu.make_async_copy(w_up.at[pl.ds(row, 3072), pl.ds(col, 512)], wbuf.at[slot], wsem.at[slot])

    for k in range(NQ + 1):
        fetch_q(k).start()
    for step in range(U_SLOTS):
        fetch_up(step).start()
    here.enter()

    def norm_rows(i, carry):
        rows = pl.ds(pl.multiple_of(i * 16, 16), 16)
        v = hid[rows, :].astype(F32)
        mean = jnp.sum(v, axis=-1, keepdims=True) * (1.0 / D)
        cen = v - mean
        var = jnp.sum(cen * cen, axis=-1, keepdims=True) * (1.0 / D)
        normed[rows, :] = (cen * lax.rsqrt(var + LN_EPS) * gam[...] + bet[...]).astype(BF16)
        return carry

    lax.fori_loop(0, ROWS // 16, norm_rows, 0)

    angle = jnp.transpose(jnp.broadcast_to(pos[...].astype(F32), (ROWS, HD))) * freq[...]
    cos[...] = jnp.cos(angle)
    lanes = lax.broadcasted_iota(jnp.int32, (ROWS, HD), 1)
    sine = jnp.sin(angle)
    sin[...] = jnp.where(lanes < HD // 2, -sine, sine)

    def rotate(v):
        return (v * cos[...] + pltpu.roll(v, HD // 2, 1) * sin[...]).astype(BF16).astype(F32)

    def g_send(level, k):
        where = qkv.at[pl.ds(k * QT + here.own(QT, level), QT // PART[level])]
        return here.remote(level, where, where, gsend.at[level, k], grecv.at[level, k])

    def project(k):
        fetch_q(k).wait()
        acc = jnp.dot(normed[...], qbuf[k], preferred_element_type=F32)
        return [acc[:, h * HD:(h + 1) * HD].astype(BF16).astype(F32) for h in range(2)]

    def query(k):
        for h, v in enumerate(project(k)):
            qkv[k * QT + here.own(QT, 2) + h] = rotate(v)
        g_send(2, k).start()

    def gather(level, k):
        g_send(level, k).wait()
        if level:
            g_send(level - 1, k).start()

    def up_block(n, carry):
        fetch_up(2 * n).wait()
        s0 = lax.rem(2 * n, U_SLOTS)
        acc = jnp.dot(normed[:, :3072], wbuf[s0], preferred_element_type=F32)
        fetch_up(2 * n + 1).wait()
        acc += jnp.dot(normed[:, 3072:], wbuf[s0 + 1], preferred_element_type=F32)
        for half in range(2):
            nxt = 2 * n + half + U_SLOTS

            @pl.when(nxt < UP_STEPS)
            def _():
                fetch_up(nxt).start()

        act[:, pl.ds(pl.multiple_of(n * 512, 512), 512)] = (
            0.5 * acc * (1.0 + lax.erf(acc * (2.0 ** -0.5)))).astype(BF16)
        return carry

    def up(lo, hi):
        lax.fori_loop(lo, hi, up_block, 0)

    query(0)
    query(1)
    query(2)
    k_new, v_new = project(NQ)
    qkv[NH] = rotate(k_new)
    qkv[NH + 1] = v_new
    gather(2, 0)
    up(0, 1)
    gather(2, 1)
    gather(2, 2)
    up(1, 2)
    gather(1, 0)
    up(2, 4)
    gather(1, 1)
    up(4, 6)
    gather(1, 2)
    for k in range(NQ):
        gather(0, k)


def front_call(hidden, gam, bet, pos, freq, w_qkv, w_up):
    vm = pl.BlockSpec(memory_space=pltpu.VMEM)
    anyspace = pl.BlockSpec(memory_space=pl.ANY)
    dma = pltpu.SemaphoreType.DMA
    return pl.pallas_call(
        front_kernel,
        out_shape=(jax.ShapeDtypeStruct((NH + 2, ROWS, HD), F32), jax.ShapeDtypeStruct((ROWS, FF), BF16)),
        in_specs=[vm, vm, vm, vm, vm, anyspace, anyspace],
        out_specs=(vm, vm),
        scratch_shapes=[
            pltpu.VMEM((ROWS, D), BF16),
            pltpu.VMEM((NQ + 1, D, 256), BF16),
            pltpu.VMEM((U_SLOTS, 3072, 512), BF16),
            pltpu.VMEM((ROWS, HD), F32),
            pltpu.VMEM((ROWS, HD), F32),
            dma((NQ + 1,)), dma((U_SLOTS,)), dma((LEVELS, NQ)), dma((LEVELS, NQ)),
        ],
        compiler_params=pltpu.CompilerParams(collective_id=0, has_side_effects=True, vmem_limit_bytes=FRONT_LIMIT),
        cost_estimate=pl.CostEstimate(flops=2 * ROWS * D * (FF + 1024), bytes_accessed=2 * D * (FF + 1024), transcendentals=0),
        name='front',
    )(hidden, gam, bet, pos, freq, w_qkv, w_up)


A_ROWS = 8
A_STEPS = ROWS // A_ROWS
A_SLOTS = 6
A_AHEAD = 3


def attn_kernel(pos_ref, qkv, kc, vc, o, ml, kn, vn, kbuf, vbuf, sbuf, ebuf, isem, osem):
    i = pl.program_id(0)
    origin = lax.axis_index('sp') * SEQ

    def fetch(step):
        slot = lax.rem(step, A_SLOTS)
        rows = pl.ds(step * A_ROWS, A_ROWS)
        return (pltpu.make_async_copy(kc.at[rows], kbuf.at[slot], isem.at[0, slot]),
                pltpu.make_async_copy(vc.at[rows], vbuf.at[slot], isem.at[1, slot]))

    def flush(step):
        slot = lax.rem(step, A_SLOTS)
        rows = pl.ds(step * A_ROWS, A_ROWS)
        return (pltpu.make_async_copy(kbuf.at[slot], kn.at[rows], osem.at[0, slot]),
                pltpu.make_async_copy(vbuf.at[slot], vn.at[rows], osem.at[1, slot]))

    @pl.when(i == 0)
    def _():
        for s in range(A_AHEAD):
            for c in fetch(s):
                c.start()

    @pl.when(i >= A_AHEAD)
    def _():
        for c in flush(i - A_AHEAD):
            c.wait()

    @pl.when(i + A_AHEAD < A_STEPS)
    def _():
        for c in fetch(i + A_AHEAD):
            c.start()

    for c in fetch(i):
        c.wait()
    slot = lax.rem(i, A_SLOTS)

    for r in range(A_ROWS):
        lp = pos_ref[i * A_ROWS + r] - origin
        base = pl.multiple_of((jnp.clip(lp, 0, SEQ - 1) // 16) * 16, 16)
        hit = base + lax.broadcasted_iota(jnp.int32, (16, HD), 0) == lp
        for buf, src in ((kbuf, NH), (vbuf, NH + 1)):
            new = jnp.broadcast_to(qkv[src, r:r + 1, :], (16, HD))
            old = buf[slot, r, pl.ds(base, 16), :].astype(F32)
            buf[slot, r, pl.ds(base, 16), :] = jnp.where(hit, new, old).astype(BF16)

    for r in range(A_ROWS):
        q = qkv[0:NH, r, :].astype(BF16)
        sbuf[r] = lax.dot_general(q, kbuf[slot, r], (((1,), (1,)), ((), ())), preferred_element_type=F32)
    lane = lax.broadcasted_iota(jnp.int32, (NH, HD), 1)
    mcol = jnp.zeros((NH, HD), F32)
    lcol = jnp.zeros((NH, HD), F32)
    for r in range(A_ROWS):
        valid = lax.broadcasted_iota(jnp.int32, (NH, SEQ), 1) <= pos_ref[i * A_ROWS + r] - origin
        s = jnp.where(valid, sbuf[r], -jnp.inf)
        m = jnp.max(s, axis=-1, keepdims=True)
        m = jnp.where(m == -jnp.inf, NEG_FILL, m)
        e = jnp.exp2((s - m) * SCALE2)
        l = jnp.sum(e, axis=-1, keepdims=True)
        ebuf[r] = e.astype(BF16)
        mcol = jnp.where(lane == r, m * SCALE2, mcol)
        lcol = jnp.where(lane == r, l, lcol)
    for r in range(A_ROWS):
        o[:, r, :] = jnp.dot(ebuf[r], vbuf[slot, r], preferred_element_type=F32)
    pad = jnp.zeros((16, HD), F32)
    ml[...] = jnp.transpose(jnp.concatenate([mcol, pad, lcol, pad], axis=0))[:A_ROWS]

    for c in flush(i):
        c.start()

    @pl.when(i == A_STEPS - 1)
    def _():
        for step in range(A_STEPS - A_AHEAD, A_STEPS):
            for c in flush(step):
                c.wait()


def attn_call(positions, qkv, k_cache, v_cache):
    anyspace = pl.BlockSpec(memory_space=pl.ANY)
    cache = jax.ShapeDtypeStruct((ROWS, SEQ, HD), BF16)
    return pl.pallas_call(
        attn_kernel,
        out_shape=(jax.ShapeDtypeStruct((NH, ROWS, HD), F32), jax.ShapeDtypeStruct((ROWS, HD), F32), cache, cache),
        grid_spec=pltpu.PrefetchScalarGridSpec(
            num_scalar_prefetch=1,
            grid=(A_STEPS,),
            in_specs=[pl.BlockSpec((NH + 2, A_ROWS, HD), lambda i, p: (0, i, 0)), anyspace, anyspace],
            out_specs=(pl.BlockSpec((NH, A_ROWS, HD), lambda i, p: (0, i, 0)), pl.BlockSpec((A_ROWS, HD), lambda i, p: (i, 0)),
                       anyspace, anyspace),
            scratch_shapes=[
                pltpu.VMEM((A_SLOTS, A_ROWS, SEQ, HD), BF16),
                pltpu.VMEM((A_SLOTS, A_ROWS, SEQ, HD), BF16),
                pltpu.VMEM((A_ROWS, NH, SEQ), F32),
                pltpu.VMEM((A_ROWS, NH, SEQ), BF16),
                pltpu.SemaphoreType.DMA((2, A_SLOTS)),
                pltpu.SemaphoreType.DMA((2, A_SLOTS)),
            ]),
        compiler_params=pltpu.CompilerParams(vmem_limit_bytes=ATTN_LIMIT, dimension_semantics=('arbitrary',)),
        cost_estimate=pl.CostEstimate(flops=4 * ROWS * NH * SEQ * HD, bytes_accessed=8 * ROWS * SEQ * HD, transcendentals=0),
        name='attn',
    )(positions, qkv, k_cache, v_cache)


W_SLOTS = 6
DOWN_STEPS = 12
NR = 3
RT = NH // NR
NK = 3
CT = NH // NK
OWN = NH // 8


def tail_kernel(act, ml_in, o_in, hid, w_down, w_out, out,
                wbuf, wobuf, part, mine, orecv0, orecv1, orecv2, stats, mlr, wts,
                precv0, precv1, precv2, gath, ctx,
                wsem, wosem, osend, orecv, msend, mrecv, psend, precv, gsend, grecv):
    here = Place()
    own, other = here.own, here.other

    def fetch_down(step):
        slot = lax.rem(step, W_SLOTS)
        col = pl.multiple_of(step * 512, 512)
        return pltpu.make_async_copy(w_down.at[:, pl.ds(col, 512)], wbuf.at[slot], wsem.at[slot])

    def wo_copy(k):
        rows = pl.ds(pl.multiple_of((k * RT + own(RT, 2)) * HD, HD), RT // 8 * HD)
        return pltpu.make_async_copy(w_out.at[rows], wobuf.at[pl.ds(k * (RT // 8 * HD), RT // 8 * HD)], wosem.at[k])

    o_to = (orecv0, orecv1, orecv2)

    def o_send(level, k):
        if level == 0:
            src = o_in.at[pl.ds(k * RT + other(RT, 0), RT // 2)]
        else:
            src = mine.at[k, pl.ds(other(RT, level) - own(RT, 0), RT // PART[level])]
        return here.remote(level, src, o_to[level].at[k], osend.at[level, k], orecv.at[level, k])

    def m_send(level):
        src = ml_in if level == 0 else stats.at[level - 1]
        return here.remote(level, src, mlr.at[level], msend.at[level], mrecv.at[level])

    lanes = lax.broadcasted_iota(jnp.int32, (ROWS, HD), 1)

    def merge_stats(level):
        m_send(level).wait()
        ours = ml_in[...] if level == 0 else stats[level - 1]
        theirs = mlr[level]
        top = jnp.maximum(ours, theirs)
        w1 = jnp.exp2(ours - top)
        w2 = jnp.exp2(theirs - top)
        total = ours * pltpu.roll(w1, 64, 1) + theirs * pltpu.roll(w2, 64, 1)
        wts[level, 0] = w1
        wts[level, 1] = w2
        stats[level] = jnp.where(lanes < 64, top, total)

    def shift(v, by):
        return pltpu.roll(v, lax.rem(HD - by, HD), 1)

    def merge_heads(level, k):
        o_send(level, k).wait()
        first_head = k * RT + own(RT, level)
        w1 = shift(wts[level, 0], first_head)
        w2 = shift(wts[level, 1], first_head)
        base = own(RT, level) - own(RT, 0)
        for h in range(RT // PART[level]):
            ours = o_in[first_head + h] if level == 0 else mine[k, base + h]
            mine[k, base + h] = ours * w1[:, h:h + 1] + o_to[level][k, h] * w2[:, h:h + 1]
        if level < 2:
            if k == 0:
                m_send(level + 1).start()
            o_send(level + 1, k).start()
        else:
            l = shift(stats[2], first_head)
            for h in range(RT // 8):
                col = (k * (RT // 8) + h) * HD
                ctx[:, col:col + HD] = (mine[k, base + h] / l[:, 64 + h:65 + h]).astype(BF16)

    def down_block(n, carry):
        fetch_down(n).wait()
        acc = jnp.dot(act[...], wbuf[lax.rem(n, W_SLOTS)], preferred_element_type=F32)

        @pl.when(n + W_SLOTS < DOWN_STEPS)
        def _():
            fetch_down(n + W_SLOTS).start()

        for t in range(4):
            part[n * 4 + t] = acc[:, t * HD:(t + 1) * HD]
        return carry

    def down(lo, hi):
        lax.fori_loop(lo, hi, down_block, 0)

    p_to = (precv0, precv1, precv2)

    def p_send(level, k):
        src = part.at[pl.ds(k * CT + other(CT, level), CT // PART[level])]
        return here.remote(level, src, p_to[level].at[k], psend.at[level, k], precv.at[level, k])

    def g_send(level, k):
        where = gath.at[pl.ds(k * CT + own(CT, level), CT // PART[level])]
        return here.remote(level, where, where, gsend.at[level, k], grecv.at[level, k])

    def project(k):
        def tiles(n, carry):
            t0 = k * CT + n * 4
            acc = jnp.dot(ctx[...], wobuf[:, pl.ds(pl.multiple_of(t0 * HD, 512), 512)], preferred_element_type=F32)
            for t in range(4):
                part[t0 + t] += acc[:, t * HD:(t + 1) * HD]
            return carry

        lax.fori_loop(0, CT // 4, tiles, 0)
        p_send(0, k).start()

    def reduce(level, k):
        p_send(level, k).wait()
        base, count = k * CT + own(CT, level), CT // PART[level]
        if level < 2:
            part[pl.ds(base, count)] = part[pl.ds(base, count)] + p_to[level][k]
            p_send(level + 1, k).start()
        else:
            for t in range(count):
                col = pl.multiple_of((base + t) * HD, HD)
                total = hid[:, pl.ds(col, HD)].astype(F32) + (part[base + t] + p_to[2][k, t])
                gath[base + t] = total.astype(BF16).astype(F32)
            g_send(2, k).start()

    def gather(level, k):
        g_send(level, k).wait()
        if level > 0:
            g_send(level - 1, k).start()
        else:
            for t in range(CT):
                col = (k * CT + t) * HD
                out[:, col:col + HD] = gath[k * CT + t].astype(BF16)

    here.enter()
    m_send(0).start()
    for k in range(NR):
        o_send(0, k).start()
    for s in range(W_SLOTS):
        fetch_down(s).start()
    for k in range(NR):
        wo_copy(k).start()

    merge_stats(0)
    for k in range(NR):
        merge_heads(0, k)
    down(0, 3)
    merge_stats(1)
    merge_heads(1, 0)
    down(3, 6)
    merge_heads(1, 1)
    down(6, 9)
    merge_stats(2)
    merge_heads(2, 0)
    merge_heads(1, 2)
    down(9, 12)
    merge_heads(2, 1)
    for k in range(NR):
        wo_copy(k).wait()
    merge_heads(2, 2)
    project(0)
    project(1)
    reduce(0, 0)
    project(2)
    reduce(0, 1)
    reduce(0, 2)
    for wave in range(1, NK + 5):
        for k in range(NK):
            s = wave - k
            if 1 <= s <= 2:
                reduce(s, k)
            elif 3 <= s <= 5:
                gather(5 - s, k)


def tail_call(act, ml, o, hidden, w_down, w_out):
    vm = pl.BlockSpec(memory_space=pltpu.VMEM)
    anyspace = pl.BlockSpec(memory_space=pl.ANY)
    dma = pltpu.SemaphoreType.DMA
    return pl.pallas_call(
        tail_kernel,
        out_shape=jax.ShapeDtypeStruct((ROWS, D), BF16),
        in_specs=[vm, vm, vm, vm, anyspace, anyspace],
        out_specs=vm,
        scratch_shapes=[
            pltpu.VMEM((W_SLOTS, 3072, 512), BF16),
            pltpu.VMEM((OWN * HD, D), BF16),
            pltpu.VMEM((NH, ROWS, HD), F32),
            pltpu.VMEM((NR, RT // 2, ROWS, HD), F32),
            pltpu.VMEM((NR, RT // 2, ROWS, HD), F32),
            pltpu.VMEM((NR, RT // 4, ROWS, HD), F32),
            pltpu.VMEM((NR, RT // 8, ROWS, HD), F32),
            pltpu.VMEM((LEVELS, ROWS, HD), F32),
            pltpu.VMEM((LEVELS, ROWS, HD), F32),
            pltpu.VMEM((LEVELS, 2, ROWS, HD), F32),
            pltpu.VMEM((NK, CT // 2, ROWS, HD), F32),
            pltpu.VMEM((NK, CT // 4, ROWS, HD), F32),
            pltpu.VMEM((NK, CT // 8, ROWS, HD), F32),
            pltpu.VMEM((NH, ROWS, HD), F32),
            pltpu.VMEM((ROWS, OWN * HD), BF16),
            dma((W_SLOTS,)), dma((NR,)),
            dma((LEVELS, NR)), dma((LEVELS, NR)), dma((LEVELS,)), dma((LEVELS,)),
            dma((LEVELS, NK)), dma((LEVELS, NK)), dma((LEVELS, NK)), dma((LEVELS, NK)),
        ],
        compiler_params=pltpu.CompilerParams(collective_id=1, has_side_effects=True, vmem_limit_bytes=TAIL_LIMIT),
        cost_estimate=pl.CostEstimate(flops=2 * ROWS * D * FF, bytes_accessed=2 * D * FF, transcendentals=0),
        name='tail',
    )(act, ml, o, hidden, w_down, w_out)


def device_step(hidden, ln_gamma, ln_beta, w_qkv, w_out, w_up, w_down, k_cache, v_cache, positions):
    inv_freq = 1.0 / (ROPE_BASE ** (jnp.arange(0, HD, 2, dtype=F32) / HD))
    freq = jnp.concatenate([inv_freq, inv_freq])[None, :]
    qkv, act = front_call(hidden, ln_gamma[None, :], ln_beta[None, :], positions[None, :], freq, w_qkv, w_up)
    o, ml, k_next, v_next = attn_call(positions, qkv, k_cache, v_cache)
    out = tail_call(act, ml, o, hidden, w_down, w_out)
    return out, k_next, v_next


def solution(mesh):
    cache_spec = P('dp', 'sp', None)
    in_specs = (P('dp', None), P(None), P(None), P(None, None), P(None, None), P(None, 'sp'), P('sp', None), cache_spec, cache_spec, P('dp'))
    out_specs = (P('dp', None), cache_spec, cache_spec)
    return jax.shard_map(device_step, mesh=mesh, in_specs=in_specs, out_specs=out_specs, check_vma=False)
```

time: 123 us -> 118 us (0.959)
  Pallas kernels: 117 us -> 112 us
  other arithmetic: 2.4 us -> 0.09 us
  local copies, waits for them, and re-layouts: 2.69 us -> 4.69 us
    pallas_call x1, Pallas kernels: 68.5 us -> 62.5 us  [tail_call(): pl.pallas_call(tail_kernel, out_shape=jax.ShapeDtypeStruct((ROWS, D), BF1...]
    pallas_call x1, Pallas kernels: 19.7 us -> 25.5 us  [front_call(): pl.pallas_call(front_kernel, out_shape=(jax.ShapeDtypeStruct((NH + 2, ROW...]
    pallas_call x1, Pallas kernels: 28.6 us -> 23.8 us  [attn_call(): pl.pallas_call(attn_kernel, out_shape=(jax.ShapeDtypeStruct((NH, ROWS, HD...]
    unnamed x1 -> x11, local copies, waits for them, and re-layouts: 2.69 us -> 4.69 us
    sub x1 -> x0, other arithmetic: 1.33 us -> none  [device_step(): local_pos = positions - lax.axis_index('sp') * SEQ]
where the time goes in v3:
time: 118 us; the launch traced here: 117 us
  Pallas kernels  112 us (95%)
  local copies, waits for them, and re-layouts  4.69 us (4%)
    pallas_call x1, Pallas kernels, tail_call(): pl.pallas_call(tail_kernel, out_shape=jax.ShapeDtypeStruct((ROWS, D), BF1...  62.5 us
    pallas_call x1, Pallas kernels, front_call(): pl.pallas_call(front_kernel, out_shape=(jax.ShapeDtypeStruct((NH + 2, ROW...  25.5 us
    pallas_call x1, Pallas kernels, attn_call(): pl.pallas_call(attn_kernel, out_shape=(jax.ShapeDtypeStruct((NH, ROWS, HD...  23.8 us
    unnamed x11, local copies, waits for them, and re-layouts  4.69 us

profile of v3, /device:TPU:0, one launch (start us, length us, event | category | flops | bytes accessed | tf_op | source)
XLA Modules:
  0.0 117.3 jit_solution(15929915299860730733)
XLA Ops:
  0.6 0.1 maximum_bitcast_fusion.freq
  0.7 0.0 copy-start
  0.7 1.4 %copy-done = bf16[128,6144]{1,0:T(8,128)(2,1)S(1)} copy-done((bf16[128,6144]{1,0:T(8,128)(2,1)S(1)}, bf16[128,6144]{1,0:T(8,128)(2,1)}, u32[]{:S(2)}) %copy-start) | copy-done | bytes 1572888
  2.1 0.0 copy-start.2
  2.1 0.7 copy-done.2
  2.9 0.0 copy-start.3
  2.9 0.7 copy-done.3
  3.6 0.0 copy-start.4
  3.6 0.7 copy-done.4
  4.3 25.5 %front.1 = (f32[50,128,128]{2,1,0:T(8,128)S(1)}, bf16[128,3072]{1,0:T(8,128)(2,1)S(1)}) custom-call(bf16[128,6144]{1,0:T(8,128)(2,1)S(1)} %copy-done, f32[1,6144]{1,0:T(1,128)S(1)} %bitcast.5, f32[1,6144]{1,0:T(1,128)S(1)} %bitcast.6, s32[1,128]{1,0:T(1,128)S(1)} %bitcast.7, f32[1,128]{1,0:T(1,128)S(1)} %maximum_bitcast_fusion.freq, bf16[6144,6400]{1,0:T(8,128)(2,1)} %w.1, ...), custom_call_target="tpu_custom_call" | custom-call | flops 6442450944 | bytes 50331648 | tf_op jit(solution)/shard_map/front/pallas_call | solution.py:175
  29.8 0.0 copy-start.1
  29.8 23.8 %attn.1 = (f32[48,128,128]{2,1,0:T(8,128)S(1)}, f32[128,128]{1,0:T(8,128)S(1)}, bf16[128,512,128]{2,1,0:T(8,128)(2,1)}, bf16[128,512,128]{2,1,0:T(8,128)(2,1)}) custom-call(s32[128]{0:T(128)S(1)} %copy-done.4, f32[50,128,128]{2,1,0:T(8,128)S(1)} %get-tuple-element.10.qkv, bf16[128,512,128]{2,1,0:T(8,128)(2,1)} %kc.1, bf16[128,512,128]{2,1,0:T(8,128)(2,1)} %vc.1), custom_call_target="tpu_custom_call" | custom-call | flops 1610612736 | bytes 67108864 | tf_op jit(solution)/shard_map/attn/pallas_call | solution.py:279
  53.6 0.0 copy-done.1
  53.6 62.5 %tail.1 = bf16[128,6144]{1,0:T(8,128)(2,1)S(1)} custom-call(bf16[128,3072]{1,0:T(8,128)(2,1)S(1)} %get-tuple-element.9.act, f32[128,128]{1,0:T(8,128)S(1)} %get-tuple-element.11.ml_in, f32[48,128,128]{2,1,0:T(8,128)S(1)} %get-tuple-element.12.o_in, bf16[128,6144]{1,0:T(8,128)(2,1)S(1)} %copy-done.1, bf16[3072,6144]{1,0:T(8,128)(2,1)} %w_down.1, ...), custom_call_target="tpu_custom_call" | custom-call | flops 4831838208 | bytes 37748736 | tf_op jit(solution)/shard_map/tail/pallas_call | solution.py:479
  116.1 1.1 copy.14
  (1 shorter events, 0.0 us)
Async XLA Ops:
  0.7 1.4 %copy-start = (bf16[128,6144]{1,0:T(8,128)(2,1)S(1)}, bf16[128,6144]{1,0:T(8,128)(2,1)}, u32[]{:S(2)}) copy-start(bf16[128,6144]{1,0:T(8,128)(2,1)} %hid.3) | copy-start | bytes 4718596
  2.1 0.7 copy-start.2
  2.9 0.7 copy-start.3
  3.6 0.7 copy-start.4
  29.8 23.8 %copy-start.1 = (bf16[128,6144]{1,0:T(8,128)(2,1)S(1)}, bf16[128,6144]{1,0:T(8,128)(2,1)}, u32[]{:S(2)}) copy-start(bf16[128,6144]{1,0:T(8,128)(2,1)} %hid.3) | copy-start | bytes 4718596

commit v4 on v3

--- a/solution.py
+++ b/solution.py
@@ -70,8 +70,13 @@
 UP_STEPS = 12
 
 
-def front_kernel(hid, gam, bet, pos, freq, w, w_up, qkv, act, normed, qbuf, wbuf, cos, sin, qsem, wsem, gsend, grecv):
+def front_kernel(hid_hbm, gam_hbm, bet_hbm, pos_hbm, freq, w, w_up, qkv, act,
+                 hid, gam, bet, pos, normed, qbuf, wbuf, cos, sin, insem, qsem, wsem, gsend, grecv):
     here = Place()
+    inputs = [pltpu.make_async_copy(src, dst, insem.at[n]) for n, (src, dst) in enumerate(
+        ((hid_hbm, hid), (gam_hbm, gam), (bet_hbm, bet), (pos_hbm, pos)))]
+    for copy in inputs:
+        copy.start()
 
     def fetch_q(k):
         col = k * QT + here.own(QT, 2) if k < NQ else NH
@@ -85,9 +90,9 @@
 
     for k in range(NQ + 1):
         fetch_q(k).start()
-    for step in range(U_SLOTS):
-        fetch_up(step).start()
     here.enter()
+    for copy in inputs:
+        copy.wait()
 
     def norm_rows(i, carry):
         rows = pl.ds(pl.multiple_of(i * 16, 16), 16)
@@ -99,6 +104,8 @@
         return carry
 
     lax.fori_loop(0, ROWS // 16, norm_rows, 0)
+    for step in range(2):
+        fetch_up(step).start()
 
     angle = jnp.transpose(jnp.broadcast_to(pos[...].astype(F32), (ROWS, HD))) * freq[...]
     cos[...] = jnp.cos(angle)
@@ -149,8 +156,12 @@
         lax.fori_loop(lo, hi, up_block, 0)
 
     query(0)
+    for step in range(2, 4):
+        fetch_up(step).start()
     query(1)
     query(2)
+    for step in range(4, U_SLOTS):
+        fetch_up(step).start()
     k_new, v_new = project(NQ)
     qkv[NH] = rotate(k_new)
     qkv[NH + 1] = v_new
@@ -170,20 +181,24 @@
 
 def front_call(hidden, gam, bet, pos, freq, w_qkv, w_up):
     vm = pl.BlockSpec(memory_space=pltpu.VMEM)
-    anyspace = pl.BlockSpec(memory_space=pl.ANY)
+    hbm = pl.BlockSpec(memory_space=pltpu.HBM)
     dma = pltpu.SemaphoreType.DMA
     return pl.pallas_call(
         front_kernel,
         out_shape=(jax.ShapeDtypeStruct((NH + 2, ROWS, HD), F32), jax.ShapeDtypeStruct((ROWS, FF), BF16)),
-        in_specs=[vm, vm, vm, vm, vm, anyspace, anyspace],
+        in_specs=[hbm, hbm, hbm, hbm, vm, hbm, hbm],
         out_specs=(vm, vm),
         scratch_shapes=[
+            pltpu.VMEM((ROWS, D), BF16),
+            pltpu.VMEM((1, D), F32),
+            pltpu.VMEM((1, D), F32),
+            pltpu.VMEM((1, ROWS), jnp.int32),
             pltpu.VMEM((ROWS, D), BF16),
             pltpu.VMEM((NQ + 1, D, 256), BF16),
             pltpu.VMEM((U_SLOTS, 3072, 512), BF16),
             pltpu.VMEM((ROWS, HD), F32),
             pltpu.VMEM((ROWS, HD), F32),
-            dma((NQ + 1,)), dma((U_SLOTS,)), dma((LEVELS, NQ)), dma((LEVELS, NQ)),
+            dma((4,)), dma((NQ + 1,)), dma((U_SLOTS,)), dma((LEVELS, NQ)), dma((LEVELS, NQ)),
         ],
         compiler_params=pltpu.CompilerParams(collective_id=0, has_side_effects=True, vmem_limit_bytes=FRONT_LIMIT),
         cost_estimate=pl.CostEstimate(flops=2 * ROWS * D * (FF + 1024), bytes_accessed=2 * D * (FF + 1024), transcendentals=0),
@@ -435,33 +450,37 @@
     m_send(0).start()
     for k in range(NR):
         o_send(0, k).start()
-    for s in range(W_SLOTS):
+    for s in range(4):
         fetch_down(s).start()
-    for k in range(NR):
-        wo_copy(k).start()
 
     merge_stats(0)
     for k in range(NR):
         merge_heads(0, k)
+    for s in range(4, W_SLOTS):
+        fetch_down(s).start()
     down(0, 3)
     merge_stats(1)
     merge_heads(1, 0)
-    down(3, 6)
+    down(3, 5)
+    for k in range(NR):
+        wo_copy(k).start()
     merge_heads(1, 1)
-    down(6, 9)
     merge_stats(2)
     merge_heads(2, 0)
+    down(5, 6)
     merge_heads(1, 2)
-    down(9, 12)
     merge_heads(2, 1)
+    down(6, 8)
     for k in range(NR):
         wo_copy(k).wait()
     merge_heads(2, 2)
     project(0)
     project(1)
     reduce(0, 0)
+    down(8, 10)
+    reduce(0, 1)
+    down(10, 12)
     project(2)
-    reduce(0, 1)
     reduce(0, 2)
     for wave in range(1, NK + 5):
         for k in range(NK):
@@ -510,7 +529,9 @@
 def device_step(hidden, ln_gamma, ln_beta, w_qkv, w_out, w_up, w_down, k_cache, v_cache, positions):
     inv_freq = 1.0 / (ROPE_BASE ** (jnp.arange(0, HD, 2, dtype=F32) / HD))
     freq = jnp.concatenate([inv_freq, inv_freq])[None, :]
-    qkv, act = front_call(hidden, ln_gamma[None, :], ln_beta[None, :], positions[None, :], freq, w_qkv, w_up)
+    inputs = [pltpu.with_memory_space_constraint(v, pltpu.HBM)
+              for v in (hidden, ln_gamma[None, :], ln_beta[None, :], positions[None, :])]
+    qkv, act = front_call(*inputs, freq, w_qkv, w_up)
     o, ml, k_next, v_next = attn_call(positions, qkv, k_cache, v_cache)
     out = tail_call(act, ml, o, hidden, w_down, w_out)
     return out, k_next, v_next

time: 118 us -> 117 us (level)
  local copies, waits for them, and re-layouts: 4.69 us -> 1.16 us
  Pallas kernels: 112 us -> 115 us
    unnamed x11 -> x5, local copies, waits for them, and re-layouts: 4.69 us -> 1.16 us
    pallas_call x1, Pallas kernels: 25.5 us -> 28.4 us  [front_call(): pl.pallas_call(front_kernel, out_shape=(jax.ShapeDtypeStruct((NH + 2, ROW...]
where the time goes in v4:
time: 117 us
  Pallas kernels  115 us (98%)
    pallas_call x1, Pallas kernels, tail_call(): pl.pallas_call(tail_kernel, out_shape=jax.ShapeDtypeStruct((ROWS, D), BF1...  63 us
    pallas_call x1, Pallas kernels, front_call(): pl.pallas_call(front_kernel, out_shape=(jax.ShapeDtypeStruct((NH + 2, ROW...  28.4 us
    pallas_call x1, Pallas kernels, attn_call(): pl.pallas_call(attn_kernel, out_shape=(jax.ShapeDtypeStruct((NH, ROWS, HD...  23.8 us

profile of v4, /device:TPU:0, one launch (start us, length us, event | category | flops | bytes accessed | tf_op | source)
XLA Modules:
  0.0 117.1 jit_solution(4748390919343236137)
XLA Ops:
  0.6 0.1 maximum_bitcast_fusion.freq
  0.7 0.0 copy-start.1
  0.7 28.4 %front.1 = (f32[50,128,128]{2,1,0:T(8,128)S(1)}, bf16[128,3072]{1,0:T(8,128)(2,1)S(1)}) custom-call(bf16[128,6144]{1,0:T(8,128)(2,1)} %hid.1, f32[1,6144]{1,0:T(1,128)} %bitcast.6, f32[1,6144]{1,0:T(1,128)} %bitcast.7, s32[1,128]{1,0:T(1,128)} %bitcast.5, f32[1,128]{1,0:T(1,128)S(1)} %maximum_bitcast_fusion.freq, bf16[6144,6400]{1,0:T(8,128)(2,1)} %w.1, ...), custom_call_target="tpu_custom_call" | custom-call | flops 6442450944 | bytes 50331648 | tf_op jit(solution)/shard_map/front/pallas_call | solution.py:186
  29.1 0.0 copy-done.1
  29.2 0.0 copy-start
  29.2 23.8 %attn.1 = (f32[48,128,128]{2,1,0:T(8,128)S(1)}, f32[128,128]{1,0:T(8,128)S(1)}, bf16[128,512,128]{2,1,0:T(8,128)(2,1)}, bf16[128,512,128]{2,1,0:T(8,128)(2,1)}) custom-call(s32[128]{0:T(128)S(1)} %copy-done.1, f32[50,128,128]{2,1,0:T(8,128)S(1)} %get-tuple-element.10.qkv, bf16[128,512,128]{2,1,0:T(8,128)(2,1)} %kc.1, bf16[128,512,128]{2,1,0:T(8,128)(2,1)} %vc.1), custom_call_target="tpu_custom_call" | custom-call | flops 1610612736 | bytes 67108864 | tf_op jit(solution)/shard_map/attn/pallas_call | solution.py:294
  53.0 0.0 copy-done
  53.0 63.0 %tail.1 = bf16[128,6144]{1,0:T(8,128)(2,1)S(1)} custom-call(bf16[128,3072]{1,0:T(8,128)(2,1)S(1)} %get-tuple-element.9.act, f32[128,128]{1,0:T(8,128)S(1)} %get-tuple-element.11.ml_in, f32[48,128,128]{2,1,0:T(8,128)S(1)} %get-tuple-element.12.o_in, bf16[128,6144]{1,0:T(8,128)(2,1)S(1)} %copy-done, bf16[3072,6144]{1,0:T(8,128)(2,1)} %w_down.1, ...), custom_call_target="tpu_custom_call" | custom-call | flops 4831838208 | bytes 37748736 | tf_op jit(solution)/shard_map/tail/pallas_call | solution.py:498
  116.0 1.1 copy.14
  (1 shorter events, 0.0 us)
Async XLA Ops:
  0.7 28.4 %copy-start.1 = (s32[128]{0:T(128)S(1)}, s32[128]{0:T(128)}, u32[]{:S(2)}) copy-start(s32[128]{0:T(128)} %pos_ref.1) | copy-start | bytes 1540
  29.2 23.8 %copy-start = (bf16[128,6144]{1,0:T(8,128)(2,1)S(1)}, bf16[128,6144]{1,0:T(8,128)(2,1)}, u32[]{:S(2)}) copy-start(bf16[128,6144]{1,0:T(8,128)(2,1)} %hid.1) | copy-start | bytes 4718596

commit v5 on v4

--- a/solution.py
+++ b/solution.py
@@ -53,34 +53,47 @@
         return pltpu.make_async_remote_copy(src_ref=src, dst_ref=dst, send_sem=send, recv_sem=recv,
                                             device_id=self.peers[level], device_id_type=MESH)
 
-    def enter(self):
-        barrier = pltpu.get_barrier_semaphore()
+    def arrive(self):
         for peer in self.peers:
-            pl.semaphore_signal(barrier, inc=1, device_id=peer, device_id_type=MESH)
-        pl.semaphore_wait(barrier, len(self.peers))
+            pl.semaphore_signal(pltpu.get_barrier_semaphore(), inc=1, device_id=peer, device_id_type=MESH)
+
+    def meet(self):
+        pl.semaphore_wait(pltpu.get_barrier_semaphore(), len(self.peers))
 
 
 PART = (2, 4, 8)
 LEVELS = 3
-
-
-NQ = 3
-QT = NH // NQ
+SIZE = (8, 16, 16, 8)
+BASE = (0, 8, 24, 40)
+CHUNKS = len(SIZE)
+
+
+def span(k, level):
+    return pl.ds(BASE[k] // PART[level], SIZE[k] // PART[level])
+
+
 U_SLOTS = 6
+OWN = NH // 8
 UP_STEPS = 12
 
 
 def front_kernel(hid_hbm, gam_hbm, bet_hbm, pos_hbm, freq, w, w_up, qkv, act,
-                 hid, gam, bet, pos, normed, qbuf, wbuf, cos, sin, insem, qsem, wsem, gsend, grecv):
+                 hid, gam, bet, pos, normed, qbuf, kvbuf, wbuf, cos, sin, insem, qsem, wsem, gsend, grecv):
     here = Place()
     inputs = [pltpu.make_async_copy(src, dst, insem.at[n]) for n, (src, dst) in enumerate(
-        ((hid_hbm, hid), (gam_hbm, gam), (bet_hbm, bet), (pos_hbm, pos)))]
+        ((pos_hbm, pos), (hid_hbm, hid), (gam_hbm, gam), (bet_hbm, bet)))]
     for copy in inputs:
         copy.start()
+    here.arrive()
+
+    def part_of(k):
+        return pl.ds(BASE[k] // 8 * HD, SIZE[k] // 8 * HD)
 
     def fetch_q(k):
-        col = k * QT + here.own(QT, 2) if k < NQ else NH
-        return pltpu.make_async_copy(w.at[:, pl.ds(pl.multiple_of(col * HD, 256), 256)], qbuf.at[k], qsem.at[k])
+        if k == CHUNKS:
+            return pltpu.make_async_copy(w.at[:, pl.ds(NH * HD, 2 * HD)], kvbuf, qsem.at[k])
+        col = pl.multiple_of((BASE[k] + here.own(SIZE[k], 2)) * HD, HD)
+        return pltpu.make_async_copy(w.at[:, pl.ds(col, SIZE[k] // 8 * HD)], qbuf.at[:, part_of(k)], qsem.at[k])
 
     def fetch_up(step):
         slot = lax.rem(step, U_SLOTS)
@@ -88,11 +101,15 @@
         row = pl.multiple_of(lax.rem(step, 2) * 3072, 3072)
         return pltpu.make_async_copy(w_up.at[pl.ds(row, 3072), pl.ds(col, 512)], wbuf.at[slot], wsem.at[slot])
 
-    for k in range(NQ + 1):
+    for k in range(CHUNKS + 1):
         fetch_q(k).start()
-    here.enter()
-    for copy in inputs:
-        copy.wait()
+
+    inputs[0].wait()
+    angle = jnp.transpose(jnp.broadcast_to(pos[...].astype(F32), (ROWS, HD))) * freq[...]
+    cos[...] = jnp.cos(angle)
+    lanes = lax.broadcasted_iota(jnp.int32, (ROWS, HD), 1)
+    sine = jnp.sin(angle)
+    sin[...] = jnp.where(lanes < HD // 2, -sine, sine)
 
     def norm_rows(i, carry):
         rows = pl.ds(pl.multiple_of(i * 16, 16), 16)
@@ -103,32 +120,33 @@
         normed[rows, :] = (cen * lax.rsqrt(var + LN_EPS) * gam[...] + bet[...]).astype(BF16)
         return carry
 
-    lax.fori_loop(0, ROWS // 16, norm_rows, 0)
+    for copy in inputs[1:]:
+        copy.wait()
     for step in range(2):
         fetch_up(step).start()
-
-    angle = jnp.transpose(jnp.broadcast_to(pos[...].astype(F32), (ROWS, HD))) * freq[...]
-    cos[...] = jnp.cos(angle)
-    lanes = lax.broadcasted_iota(jnp.int32, (ROWS, HD), 1)
-    sine = jnp.sin(angle)
-    sin[...] = jnp.where(lanes < HD // 2, -sine, sine)
+    lax.fori_loop(0, ROWS // 16, norm_rows, 0, unroll=4)
+    here.meet()
 
     def rotate(v):
         return (v * cos[...] + pltpu.roll(v, HD // 2, 1) * sin[...]).astype(BF16).astype(F32)
 
     def g_send(level, k):
-        where = qkv.at[pl.ds(k * QT + here.own(QT, level), QT // PART[level])]
+        where = qkv.at[pl.ds(BASE[k] + here.own(SIZE[k], level), SIZE[k] // PART[level])]
         return here.remote(level, where, where, gsend.at[level, k], grecv.at[level, k])
 
-    def project(k):
-        fetch_q(k).wait()
-        acc = jnp.dot(normed[...], qbuf[k], preferred_element_type=F32)
-        return [acc[:, h * HD:(h + 1) * HD].astype(BF16).astype(F32) for h in range(2)]
-
-    def query(k):
-        for h, v in enumerate(project(k)):
-            qkv[k * QT + here.own(QT, 2) + h] = rotate(v)
-        g_send(2, k).start()
+    def project(weights):
+        acc = jnp.dot(normed[...], weights[...], preferred_element_type=F32)
+        return [acc[:, h:h + HD].astype(BF16).astype(F32) for h in range(0, acc.shape[1], HD)]
+
+    def queries(chunks):
+        for k in chunks:
+            fetch_q(k).wait()
+        first = BASE[chunks[0]] // 8
+        heads = project(qbuf.at[:, pl.ds(first * HD, OWN // 2 * HD)])
+        for k in chunks:
+            for h in range(SIZE[k] // 8):
+                qkv[BASE[k] + here.own(SIZE[k], 2) + h] = rotate(heads[BASE[k] // 8 - first + h])
+            g_send(2, k).start()
 
     def gather(level, k):
         g_send(level, k).wait()
@@ -155,28 +173,32 @@
     def up(lo, hi):
         lax.fori_loop(lo, hi, up_block, 0)
 
-    query(0)
-    for step in range(2, 4):
+    queries((0, 1))
+    queries((2, 3))
+    for step in range(2, U_SLOTS):
         fetch_up(step).start()
-    query(1)
-    query(2)
-    for step in range(4, U_SLOTS):
-        fetch_up(step).start()
-    k_new, v_new = project(NQ)
+    fetch_q(CHUNKS).wait()
+    k_new, v_new = project(kvbuf)
     qkv[NH] = rotate(k_new)
     qkv[NH + 1] = v_new
     gather(2, 0)
+    gather(2, 1)
     up(0, 1)
-    gather(2, 1)
     gather(2, 2)
     up(1, 2)
+    gather(2, 3)
     gather(1, 0)
-    up(2, 4)
+    up(2, 3)
+    gather(0, 0)
     gather(1, 1)
-    up(4, 6)
+    up(3, 4)
+    gather(0, 1)
+    up(4, 5)
     gather(1, 2)
-    for k in range(NQ):
-        gather(0, k)
+    gather(1, 3)
+    up(5, 6)
+    gather(0, 2)
+    gather(0, 3)
 
 
 def front_call(hidden, gam, bet, pos, freq, w_qkv, w_up):
@@ -194,11 +216,12 @@
             pltpu.VMEM((1, D), F32),
             pltpu.VMEM((1, ROWS), jnp.int32),
             pltpu.VMEM((ROWS, D), BF16),
-            pltpu.VMEM((NQ + 1, D, 256), BF16),
+            pltpu.VMEM((D, OWN * HD), BF16),
+            pltpu.VMEM((D, 2 * HD), BF16),
             pltpu.VMEM((U_SLOTS, 3072, 512), BF16),
             pltpu.VMEM((ROWS, HD), F32),
             pltpu.VMEM((ROWS, HD), F32),
-            dma((4,)), dma((NQ + 1,)), dma((U_SLOTS,)), dma((LEVELS, NQ)), dma((LEVELS, NQ)),
+            dma((4,)), dma((CHUNKS + 1,)), dma((U_SLOTS,)), dma((LEVELS, CHUNKS)), dma((LEVELS, CHUNKS)),
         ],
         compiler_params=pltpu.CompilerParams(collective_id=0, has_side_effects=True, vmem_limit_bytes=FRONT_LIMIT),
         cost_estimate=pl.CostEstimate(flops=2 * ROWS * D * (FF + 1024), bytes_accessed=2 * D * (FF + 1024), transcendentals=0),
@@ -316,11 +339,8 @@
 
 W_SLOTS = 6
 DOWN_STEPS = 12
-NR = 3
-RT = NH // NR
-NK = 3
-CT = NH // NK
-OWN = NH // 8
+ORDER = ((0, 0), (1, 0), (0, 1), (2, 0), (1, 1), (3, 0), (2, 1), (3, 1), (0, 2), (1, 2), (0, 3), (2, 2), (1, 3), (3, 2),
+         (0, 4), (2, 3), (1, 4), (3, 3), (0, 5), (2, 4), (0, 6), (3, 4), (1, 5), (1, 6), (2, 5), (3, 5), (2, 6), (3, 6))
 
 
 def tail_kernel(act, ml_in, o_in, hid, w_down, w_out, out,
@@ -336,17 +356,18 @@
         return pltpu.make_async_copy(w_down.at[:, pl.ds(col, 512)], wbuf.at[slot], wsem.at[slot])
 
     def wo_copy(k):
-        rows = pl.ds(pl.multiple_of((k * RT + own(RT, 2)) * HD, HD), RT // 8 * HD)
-        return pltpu.make_async_copy(w_out.at[rows], wobuf.at[pl.ds(k * (RT // 8 * HD), RT // 8 * HD)], wosem.at[k])
+        rows = pl.ds(pl.multiple_of((BASE[k] + own(SIZE[k], 2)) * HD, HD), SIZE[k] // 8 * HD)
+        return pltpu.make_async_copy(w_out.at[rows], wobuf.at[pl.ds(BASE[k] // 8 * HD, SIZE[k] // 8 * HD)], wosem.at[k])
 
     o_to = (orecv0, orecv1, orecv2)
 
+    def mine_at(k, start):
+        return BASE[k] // 2 + start - own(SIZE[k], 0)
+
     def o_send(level, k):
-        if level == 0:
-            src = o_in.at[pl.ds(k * RT + other(RT, 0), RT // 2)]
-        else:
-            src = mine.at[k, pl.ds(other(RT, level) - own(RT, 0), RT // PART[level])]
-        return here.remote(level, src, o_to[level].at[k], osend.at[level, k], orecv.at[level, k])
+        start, count = other(SIZE[k], level), SIZE[k] // PART[level]
+        src = mine.at[pl.ds(mine_at(k, start), count)] if level else o_in.at[pl.ds(BASE[k] + start, count)]
+        return here.remote(level, src, o_to[level].at[span(k, level)], osend.at[level, k], orecv.at[level, k])
 
     def m_send(level):
         src = ml_in if level == 0 else stats.at[level - 1]
@@ -370,23 +391,25 @@
         return pltpu.roll(v, lax.rem(HD - by, HD), 1)
 
     def merge_heads(level, k):
+        if k == 0:
+            merge_stats(level)
         o_send(level, k).wait()
-        first_head = k * RT + own(RT, level)
-        w1 = shift(wts[level, 0], first_head)
-        w2 = shift(wts[level, 1], first_head)
-        base = own(RT, level) - own(RT, 0)
-        for h in range(RT // PART[level]):
-            ours = o_in[first_head + h] if level == 0 else mine[k, base + h]
-            mine[k, base + h] = ours * w1[:, h:h + 1] + o_to[level][k, h] * w2[:, h:h + 1]
+        start = own(SIZE[k], level)
+        w1 = shift(wts[level, 0], BASE[k] + start)
+        w2 = shift(wts[level, 1], BASE[k] + start)
+        base = mine_at(k, start)
+        for h in range(SIZE[k] // PART[level]):
+            ours = mine[base + h] if level else o_in[BASE[k] + start + h]
+            mine[base + h] = ours * w1[:, h:h + 1] + o_to[level][BASE[k] // PART[level] + h] * w2[:, h:h + 1]
         if level < 2:
             if k == 0:
                 m_send(level + 1).start()
             o_send(level + 1, k).start()
         else:
-            l = shift(stats[2], first_head)
-            for h in range(RT // 8):
-                col = (k * (RT // 8) + h) * HD
-                ctx[:, col:col + HD] = (mine[k, base + h] / l[:, 64 + h:65 + h]).astype(BF16)
+            l = shift(stats[2], BASE[k] + start)
+            for h in range(SIZE[k] // 8):
+                col = (BASE[k] // 8 + h) * HD
+                ctx[:, col:col + HD] = (mine[base + h] / l[:, 64 + h:65 + h]).astype(BF16)
 
     def down_block(n, carry):
         fetch_down(n).wait()
@@ -406,34 +429,34 @@
     p_to = (precv0, precv1, precv2)
 
     def p_send(level, k):
-        src = part.at[pl.ds(k * CT + other(CT, level), CT // PART[level])]
-        return here.remote(level, src, p_to[level].at[k], psend.at[level, k], precv.at[level, k])
+        src = part.at[pl.ds(BASE[k] + other(SIZE[k], level), SIZE[k] // PART[level])]
+        return here.remote(level, src, p_to[level].at[span(k, level)], psend.at[level, k], precv.at[level, k])
 
     def g_send(level, k):
-        where = gath.at[pl.ds(k * CT + own(CT, level), CT // PART[level])]
+        where = gath.at[pl.ds(BASE[k] + own(SIZE[k], level), SIZE[k] // PART[level])]
         return here.remote(level, where, where, gsend.at[level, k], grecv.at[level, k])
 
     def project(k):
         def tiles(n, carry):
-            t0 = k * CT + n * 4
+            t0 = BASE[k] + n * 4
             acc = jnp.dot(ctx[...], wobuf[:, pl.ds(pl.multiple_of(t0 * HD, 512), 512)], preferred_element_type=F32)
             for t in range(4):
                 part[t0 + t] += acc[:, t * HD:(t + 1) * HD]
             return carry
 
-        lax.fori_loop(0, CT // 4, tiles, 0)
+        lax.fori_loop(0, SIZE[k] // 4, tiles, 0)
         p_send(0, k).start()
 
     def reduce(level, k):
         p_send(level, k).wait()
-        base, count = k * CT + own(CT, level), CT // PART[level]
+        base, count = BASE[k] + own(SIZE[k], level), SIZE[k] // PART[level]
         if level < 2:
-            part[pl.ds(base, count)] = part[pl.ds(base, count)] + p_to[level][k]
+            part[pl.ds(base, count)] = part[pl.ds(base, count)] + p_to[level][span(k, level)]
             p_send(level + 1, k).start()
         else:
             for t in range(count):
                 col = pl.multiple_of((base + t) * HD, HD)
-                total = hid[:, pl.ds(col, HD)].astype(F32) + (part[base + t] + p_to[2][k, t])
+                total = hid[:, pl.ds(col, HD)].astype(F32) + (part[base + t] + p_to[2][BASE[k] // 8 + t])
                 gath[base + t] = total.astype(BF16).astype(F32)
             g_send(2, k).start()
 
@@ -442,53 +465,44 @@
         if level > 0:
             g_send(level - 1, k).start()
         else:
-            for t in range(CT):
-                col = (k * CT + t) * HD
-                out[:, col:col + HD] = gath[k * CT + t].astype(BF16)
-
-    here.enter()
-    m_send(0).start()
-    for k in range(NR):
-        o_send(0, k).start()
+            for t in range(BASE[k], BASE[k] + SIZE[k]):
+                out[:, t * HD:(t + 1) * HD] = gath[t].astype(BF16)
+
+    here.arrive()
     for s in range(4):
         fetch_down(s).start()
-
-    merge_stats(0)
-    for k in range(NR):
+    here.meet()
+    m_send(0).start()
+    for k in range(CHUNKS):
+        o_send(0, k).start()
+    for k in range(CHUNKS):
         merge_heads(0, k)
     for s in range(4, W_SLOTS):
         fetch_down(s).start()
-    down(0, 3)
-    merge_stats(1)
+    down(0, 2)
     merge_heads(1, 0)
-    down(3, 5)
-    for k in range(NR):
+    down(2, 6)
+    for k in range(CHUNKS):
         wo_copy(k).start()
     merge_heads(1, 1)
-    merge_stats(2)
     merge_heads(2, 0)
-    down(5, 6)
+    down(6, 8)
     merge_heads(1, 2)
+    down(8, 10)
+    merge_heads(1, 3)
     merge_heads(2, 1)
-    down(6, 8)
-    for k in range(NR):
+    merge_heads(2, 2)
+    down(10, 12)
+    for k in range(CHUNKS):
         wo_copy(k).wait()
-    merge_heads(2, 2)
-    project(0)
-    project(1)
-    reduce(0, 0)
-    down(8, 10)
-    reduce(0, 1)
-    down(10, 12)
-    project(2)
-    reduce(0, 2)
-    for wave in range(1, NK + 5):
-        for k in range(NK):
-            s = wave - k
-            if 1 <= s <= 2:
-                reduce(s, k)
-            elif 3 <= s <= 5:
-                gather(5 - s, k)
+    merge_heads(2, 3)
+    for k, stage in ORDER:
+        if stage == 0:
+            project(k)
+        elif stage <= 3:
+            reduce(stage - 1, k)
+        else:
+            gather(6 - stage, k)
 
 
 def tail_call(act, ml, o, hidden, w_down, w_out):
@@ -504,21 +518,21 @@
             pltpu.VMEM((W_SLOTS, 3072, 512), BF16),
             pltpu.VMEM((OWN * HD, D), BF16),
             pltpu.VMEM((NH, ROWS, HD), F32),
-            pltpu.VMEM((NR, RT // 2, ROWS, HD), F32),
-            pltpu.VMEM((NR, RT // 2, ROWS, HD), F32),
-            pltpu.VMEM((NR, RT // 4, ROWS, HD), F32),
-            pltpu.VMEM((NR, RT // 8, ROWS, HD), F32),
+            pltpu.VMEM((NH // 2, ROWS, HD), F32),
+            pltpu.VMEM((NH // 2, ROWS, HD), F32),
+            pltpu.VMEM((NH // 4, ROWS, HD), F32),
+            pltpu.VMEM((NH // 8, ROWS, HD), F32),
             pltpu.VMEM((LEVELS, ROWS, HD), F32),
             pltpu.VMEM((LEVELS, ROWS, HD), F32),
             pltpu.VMEM((LEVELS, 2, ROWS, HD), F32),
-            pltpu.VMEM((NK, CT // 2, ROWS, HD), F32),
-            pltpu.VMEM((NK, CT // 4, ROWS, HD), F32),
-            pltpu.VMEM((NK, CT // 8, ROWS, HD), F32),
+            pltpu.VMEM((NH // 2, ROWS, HD), F32),
+            pltpu.VMEM((NH // 4, ROWS, HD), F32),
+            pltpu.VMEM((NH // 8, ROWS, HD), F32),
             pltpu.VMEM((NH, ROWS, HD), F32),
             pltpu.VMEM((ROWS, OWN * HD), BF16),
-            dma((W_SLOTS,)), dma((NR,)),
-            dma((LEVELS, NR)), dma((LEVELS, NR)), dma((LEVELS,)), dma((LEVELS,)),
-            dma((LEVELS, NK)), dma((LEVELS, NK)), dma((LEVELS, NK)), dma((LEVELS, NK)),
+            dma((W_SLOTS,)), dma((CHUNKS,)),
+            dma((LEVELS, CHUNKS)), dma((LEVELS, CHUNKS)), dma((LEVELS,)), dma((LEVELS,)),
+            dma((LEVELS, CHUNKS)), dma((LEVELS, CHUNKS)), dma((LEVELS, CHUNKS)), dma((LEVELS, CHUNKS)),
         ],
         compiler_params=pltpu.CompilerParams(collective_id=1, has_side_effects=True, vmem_limit_bytes=TAIL_LIMIT),
         cost_estimate=pl.CostEstimate(flops=2 * ROWS * D * FF, bytes_accessed=2 * D * FF, transcendentals=0),

time: 117 us -> 108 us (0.923)
  Pallas kernels: 115 us -> 106 us
    pallas_call x1, Pallas kernels: 63 us -> 57.4 us  [tail_call(): pl.pallas_call(tail_kernel, out_shape=jax.ShapeDtypeStruct((ROWS, D), BF1...]
    pallas_call x1, Pallas kernels: 28.4 us -> 24.6 us  [front_call(): pl.pallas_call(front_kernel, out_shape=(jax.ShapeDtypeStruct((NH + 2, ROW...]
where the time goes in v5:
time: 108 us
  Pallas kernels  106 us (98%)
  local copies, waits for them, and re-layouts  1.16 us (1%)
    pallas_call x1, Pallas kernels, tail_call(): pl.pallas_call(tail_kernel, out_shape=jax.ShapeDtypeStruct((ROWS, D), BF1...  57.4 us
    pallas_call x1, Pallas kernels, front_call(): pl.pallas_call(front_kernel, out_shape=(jax.ShapeDtypeStruct((NH + 2, ROW...  24.6 us
    pallas_call x1, Pallas kernels, attn_call(): pl.pallas_call(attn_kernel, out_shape=(jax.ShapeDtypeStruct((NH, ROWS, HD...  23.8 us

profile of v5, /device:TPU:0, one launch (start us, length us, event | category | flops | bytes accessed | tf_op | source)
XLA Modules:
  0.0 107.7 jit_solution(4952959058154615441)
XLA Ops:
  0.6 0.1 maximum_bitcast_fusion.freq
  0.7 0.0 copy-start.1
  0.7 24.6 %front.1 = (f32[50,128,128]{2,1,0:T(8,128)S(1)}, bf16[128,3072]{1,0:T(8,128)(2,1)S(1)}) custom-call(bf16[128,6144]{1,0:T(8,128)(2,1)} %hid.1, f32[1,6144]{1,0:T(1,128)} %bitcast.6, f32[1,6144]{1,0:T(1,128)} %bitcast.7, s32[1,128]{1,0:T(1,128)} %bitcast.5, f32[1,128]{1,0:T(1,128)S(1)} %maximum_bitcast_fusion.freq, bf16[6144,6400]{1,0:T(8,128)(2,1)} %w.1, ...), custom_call_target="tpu_custom_call" | custom-call | flops 6442450944 | bytes 50331648 | tf_op jit(solution)/shard_map/front/pallas_call | solution.py:208
  25.3 0.0 copy-done.1
  25.3 0.0 copy-start
  25.3 23.8 %attn.1 = (f32[48,128,128]{2,1,0:T(8,128)S(1)}, f32[128,128]{1,0:T(8,128)S(1)}, bf16[128,512,128]{2,1,0:T(8,128)(2,1)}, bf16[128,512,128]{2,1,0:T(8,128)(2,1)}) custom-call(s32[128]{0:T(128)S(1)} %copy-done.1, f32[50,128,128]{2,1,0:T(8,128)S(1)} %get-tuple-element.10.qkv, bf16[128,512,128]{2,1,0:T(8,128)(2,1)} %kc.1, bf16[128,512,128]{2,1,0:T(8,128)(2,1)} %vc.1), custom_call_target="tpu_custom_call" | custom-call | flops 1610612736 | bytes 67108864 | tf_op jit(solution)/shard_map/attn/pallas_call | solution.py:317
  49.1 0.0 copy-done
  49.1 57.4 %tail.1 = bf16[128,6144]{1,0:T(8,128)(2,1)S(1)} custom-call(bf16[128,3072]{1,0:T(8,128)(2,1)S(1)} %get-tuple-element.9.act, f32[128,128]{1,0:T(8,128)S(1)} %get-tuple-element.11.ml_in, f32[48,128,128]{2,1,0:T(8,128)S(1)} %get-tuple-element.12.o_in, bf16[128,6144]{1,0:T(8,128)(2,1)S(1)} %copy-done, bf16[3072,6144]{1,0:T(8,128)(2,1)} %w_down.1, ...), custom_call_target="tpu_custom_call" | custom-call | flops 4831838208 | bytes 37748736 | tf_op jit(solution)/shard_map/tail/pallas_call | solution.py:512
  106.5 1.1 %copy.14 = bf16[128,6144]{1,0:T(8,128)(2,1)} copy(bf16[128,6144]{1,0:T(8,128)(2,1)S(1)} %tail.1) | data formatting | bytes 3145728
  (1 shorter events, 0.0 us)
Async XLA Ops:
  0.7 24.6 %copy-start.1 = (s32[128]{0:T(128)S(1)}, s32[128]{0:T(128)}, u32[]{:S(2)}) copy-start(s32[128]{0:T(128)} %pos_ref.1) | copy-start | bytes 1540
  25.3 23.8 %copy-start = (bf16[128,6144]{1,0:T(8,128)(2,1)S(1)}, bf16[128,6144]{1,0:T(8,128)(2,1)}, u32[]{:S(2)}) copy-start(bf16[128,6144]{1,0:T(8,128)(2,1)} %hid.1) | copy-start | bytes 4718596

commit v6 on v5

--- a/solution.py
+++ b/solution.py
@@ -14,7 +14,7 @@
 MESH = pl.DeviceIdType.MESH
 FRONT_LIMIT = 46_000_000
 ATTN_LIMIT = 40_000_000
-TAIL_LIMIT = 48_500_000
+TAIL_LIMIT = 47_000_000
 
 ROWS = 128
 D = 6144
@@ -36,6 +36,7 @@
         core = lax.rem(sp, 2)
         x = lax.rem(sp // 2, 2)
         y = sp // 4
+        self.x, self.y = x, y
         first = 1 - core
         x_peer = device(y, 1 - x, core)['sp']
         y_peer = device(1 - y, x, core)['sp']
@@ -337,27 +338,36 @@
     )(positions, qkv, k_cache, v_cache)
 
 
-W_SLOTS = 6
+W_SLOTS = 5
 DOWN_STEPS = 12
-ORDER = ((0, 0), (1, 0), (0, 1), (2, 0), (1, 1), (3, 0), (2, 1), (3, 1), (0, 2), (1, 2), (0, 3), (2, 2), (1, 3), (3, 2),
-         (0, 4), (2, 3), (1, 4), (3, 3), (0, 5), (2, 4), (0, 6), (3, 4), (1, 5), (1, 6), (2, 5), (3, 5), (2, 6), (3, 6))
+F_CHUNKS = 6
+HALF = NH // 2
+ORDER = ((0, 0), (1, 0), (2, 0), (3, 0), (4, 0), (5, 0), (0, 2), (1, 2), (2, 2), (0, 3), (3, 2), (1, 3),
+         (2, 3), (4, 2), (0, 4), (5, 2), (3, 3), (1, 4), (2, 4), (4, 3), (0, 5), (5, 3), (0, 6), (3, 4),
+         (1, 5), (4, 4), (1, 6), (5, 4), (2, 5), (3, 5), (2, 6), (4, 5), (3, 6), (4, 6), (5, 5), (5, 6))
 
 
 def tail_kernel(act, ml_in, o_in, hid, w_down, w_out, out,
                 wbuf, wobuf, part, mine, orecv0, orecv1, orecv2, stats, mlr, wts,
-                precv0, precv1, precv2, gath, ctx,
-                wsem, wosem, osend, orecv, msend, mrecv, psend, precv, gsend, grecv):
+                precv0, precv1, precv2, gath, ctxf, ctx,
+                wsem, wosem, osend, orecv, msend, mrecv, csend, crecv, psend, precv, gsend, grecv):
     here = Place()
     own, other = here.own, here.other
 
     def fetch_down(step):
         slot = lax.rem(step, W_SLOTS)
-        col = pl.multiple_of(step * 512, 512)
+        col = pl.multiple_of((lax.rem(step, 2) * F_CHUNKS + step // 2) * 512, 512)
         return pltpu.make_async_copy(w_down.at[:, pl.ds(col, 512)], wbuf.at[slot], wsem.at[slot])
 
-    def wo_copy(k):
-        rows = pl.ds(pl.multiple_of((BASE[k] + own(SIZE[k], 2)) * HD, HD), SIZE[k] // 8 * HD)
-        return pltpu.make_async_copy(w_out.at[rows], wobuf.at[pl.ds(BASE[k] // 8 * HD, SIZE[k] // 8 * HD)], wosem.at[k])
+    def head_at(core, k):
+        turn = (here.x, here.y) if core == 0 else (here.y, here.x)
+        return BASE[k] + core * (SIZE[k] // 2) + turn[0] * (SIZE[k] // 4) + turn[1] * (SIZE[k] // 8)
+
+    def wo_copy(core, k):
+        rows = pl.ds(pl.multiple_of(head_at(core, k) * HD, HD), SIZE[k] // 8 * HD)
+        cols = pl.ds(pl.multiple_of(here.sides[0] * (HALF * HD), HALF * HD), HALF * HD)
+        dst = wobuf.at[pl.ds((core * OWN + BASE[k] // 8) * HD, SIZE[k] // 8 * HD)]
+        return pltpu.make_async_copy(w_out.at[rows, cols], dst, wosem.at[core, k])
 
     o_to = (orecv0, orecv1, orecv2)
 
@@ -389,6 +399,10 @@
 
     def shift(v, by):
         return pltpu.roll(v, lax.rem(HD - by, HD), 1)
+
+    def c_send(k):
+        where = ctxf.at[pl.ds(here.sides[0] * OWN + BASE[k] // 8, SIZE[k] // 8)]
+        return here.remote(0, where, where, csend.at[k], crecv.at[k])
 
     def merge_heads(level, k):
         if k == 0:
@@ -408,56 +422,63 @@
         else:
             l = shift(stats[2], BASE[k] + start)
             for h in range(SIZE[k] // 8):
-                col = (BASE[k] // 8 + h) * HD
-                ctx[:, col:col + HD] = (mine[base + h] / l[:, 64 + h:65 + h]).astype(BF16)
-
-    def down_block(n, carry):
-        fetch_down(n).wait()
-        acc = jnp.dot(act[...], wbuf[lax.rem(n, W_SLOTS)], preferred_element_type=F32)
-
-        @pl.when(n + W_SLOTS < DOWN_STEPS)
-        def _():
-            fetch_down(n + W_SLOTS).start()
-
+                value = (mine[base + h] / l[:, 64 + h:65 + h]).astype(BF16)
+                ctxf[here.sides[0] * OWN + BASE[k] // 8 + h] = value.astype(F32)
+            c_send(k).start()
+
+    def d_send(k):
+        src = part.at[pl.ds((1 - here.sides[0]) * HALF + 4 * k, 4)]
+        return here.remote(0, src, precv0.at[pl.ds(4 * k, 4)], psend.at[0, k], precv.at[0, k])
+
+    def down_pair(k, carry):
+        for side in range(2):
+            n = 2 * k + side
+            fetch_down(n).wait()
+            acc = jnp.dot(act[...], wbuf[lax.rem(n, W_SLOTS)], preferred_element_type=F32)
+
+            @pl.when(n + W_SLOTS < DOWN_STEPS)
+            def _():
+                fetch_down(n + W_SLOTS).start()
+
+            for t in range(4):
+                part[side * HALF + 4 * k + t] = acc[:, t * HD:(t + 1) * HD]
+        d_send(k).start()
+        return carry
+
+    def down(lo, hi):
+        lax.fori_loop(lo, hi, down_pair, 0)
+
+    p_to = (precv0, precv1, precv2)
+
+    def tile(k, level):
+        return here.sides[0] * HALF + 4 * k + own(8, level) - own(8, 0)
+
+    def p_send(level, k):
+        count = 8 // PART[level]
+        src = part.at[pl.ds(here.sides[0] * HALF + 4 * k + other(8, level) - own(8, 0), count)]
+        return here.remote(level, src, p_to[level].at[pl.ds(k * count, count)], psend.at[level, k], precv.at[level, k])
+
+    def g_send(level, k):
+        where = gath.at[pl.ds(tile(k, level), 8 // PART[level])]
+        return here.remote(level, where, where, gsend.at[level, k], grecv.at[level, k])
+
+    def project(k):
+        d_send(k).wait()
+        acc = jnp.dot(ctx[...], wobuf[:, k * 512:(k + 1) * 512], preferred_element_type=F32)
         for t in range(4):
-            part[n * 4 + t] = acc[:, t * HD:(t + 1) * HD]
-        return carry
-
-    def down(lo, hi):
-        lax.fori_loop(lo, hi, down_block, 0)
-
-    p_to = (precv0, precv1, precv2)
-
-    def p_send(level, k):
-        src = part.at[pl.ds(BASE[k] + other(SIZE[k], level), SIZE[k] // PART[level])]
-        return here.remote(level, src, p_to[level].at[span(k, level)], psend.at[level, k], precv.at[level, k])
-
-    def g_send(level, k):
-        where = gath.at[pl.ds(BASE[k] + own(SIZE[k], level), SIZE[k] // PART[level])]
-        return here.remote(level, where, where, gsend.at[level, k], grecv.at[level, k])
-
-    def project(k):
-        def tiles(n, carry):
-            t0 = BASE[k] + n * 4
-            acc = jnp.dot(ctx[...], wobuf[:, pl.ds(pl.multiple_of(t0 * HD, 512), 512)], preferred_element_type=F32)
-            for t in range(4):
-                part[t0 + t] += acc[:, t * HD:(t + 1) * HD]
-            return carry
-
-        lax.fori_loop(0, SIZE[k] // 4, tiles, 0)
-        p_send(0, k).start()
+            part[tile(k, 0) + t] = (part[tile(k, 0) + t] + precv0[4 * k + t]) + acc[:, t * HD:(t + 1) * HD]
+        p_send(1, k).start()
 
     def reduce(level, k):
         p_send(level, k).wait()
-        base, count = BASE[k] + own(SIZE[k], level), SIZE[k] // PART[level]
+        base, count = tile(k, level), 8 // PART[level]
         if level < 2:
-            part[pl.ds(base, count)] = part[pl.ds(base, count)] + p_to[level][span(k, level)]
+            part[pl.ds(base, count)] = part[pl.ds(base, count)] + p_to[level][pl.ds(k * count, count)]
             p_send(level + 1, k).start()
         else:
-            for t in range(count):
-                col = pl.multiple_of((base + t) * HD, HD)
-                total = hid[:, pl.ds(col, HD)].astype(F32) + (part[base + t] + p_to[2][BASE[k] // 8 + t])
-                gath[base + t] = total.astype(BF16).astype(F32)
+            col = pl.multiple_of(base * HD, HD)
+            total = hid[:, pl.ds(col, HD)].astype(F32) + (part[base] + precv2[k])
+            gath[base] = total.astype(BF16).astype(F32)
             g_send(2, k).start()
 
     def gather(level, k):
@@ -465,8 +486,9 @@
         if level > 0:
             g_send(level - 1, k).start()
         else:
-            for t in range(BASE[k], BASE[k] + SIZE[k]):
-                out[:, t * HD:(t + 1) * HD] = gath[t].astype(BF16)
+            for t in range(4 * k, 4 * k + 4):
+                for col in (t, HALF + t):
+                    out[:, col * HD:(col + 1) * HD] = gath[col].astype(BF16)
 
     here.arrive()
     for s in range(4):
@@ -479,23 +501,29 @@
         merge_heads(0, k)
     for s in range(4, W_SLOTS):
         fetch_down(s).start()
-    down(0, 2)
+    down(0, 1)
     merge_heads(1, 0)
-    down(2, 6)
-    for k in range(CHUNKS):
-        wo_copy(k).start()
+    down(1, 3)
+    for core in range(2):
+        for k in range(CHUNKS):
+            wo_copy(core, k).start()
     merge_heads(1, 1)
     merge_heads(2, 0)
-    down(6, 8)
+    down(3, 4)
     merge_heads(1, 2)
-    down(8, 10)
+    down(4, 5)
     merge_heads(1, 3)
     merge_heads(2, 1)
     merge_heads(2, 2)
-    down(10, 12)
+    down(5, 6)
+    for core in range(2):
+        for k in range(CHUNKS):
+            wo_copy(core, k).wait()
+    merge_heads(2, 3)
     for k in range(CHUNKS):
-        wo_copy(k).wait()
-    merge_heads(2, 3)
+        c_send(k).wait()
+    for h in range(2 * OWN):
+        ctx[:, h * HD:(h + 1) * HD] = ctxf[h].astype(BF16)
     for k, stage in ORDER:
         if stage == 0:
             project(k)
@@ -516,7 +544,7 @@
         out_specs=vm,
         scratch_shapes=[
             pltpu.VMEM((W_SLOTS, 3072, 512), BF16),
-            pltpu.VMEM((OWN * HD, D), BF16),
+            pltpu.VMEM((2 * OWN * HD, HALF * HD), BF16),
             pltpu.VMEM((NH, ROWS, HD), F32),
             pltpu.VMEM((NH // 2, ROWS, HD), F32),
             pltpu.VMEM((NH // 2, ROWS, HD), F32),
@@ -529,10 +557,11 @@
             pltpu.VMEM((NH // 4, ROWS, HD), F32),
             pltpu.VMEM((NH // 8, ROWS, HD), F32),
             pltpu.VMEM((NH, ROWS, HD), F32),
-            pltpu.VMEM((ROWS, OWN * HD), BF16),
-            dma((W_SLOTS,)), dma((CHUNKS,)),
-            dma((LEVELS, CHUNKS)), dma((LEVELS, CHUNKS)), dma((LEVELS,)), dma((LEVELS,)),
-            dma((LEVELS, CHUNKS)), dma((LEVELS, CHUNKS)), dma((LEVELS, CHUNKS)), dma((LEVELS, CHUNKS)),
+            pltpu.VMEM((2 * OWN, ROWS, HD), F32),
+            pltpu.VMEM((ROWS, 2 * OWN * HD), BF16),
+            dma((W_SLOTS,)), dma((2, CHUNKS)),
+            dma((LEVELS, CHUNKS)), dma((LEVELS, CHUNKS)), dma((LEVELS,)), dma((LEVELS,)), dma((CHUNKS,)), dma((CHUNKS,)),
+            dma((LEVELS, F_CHUNKS)), dma((LEVELS, F_CHUNKS)), dma((LEVELS, F_CHUNKS)), dma((LEVELS, F_CHUNKS)),
         ],
         compiler_params=pltpu.CompilerParams(collective_id=1, has_side_effects=True, vmem_limit_bytes=TAIL_LIMIT),
         cost_estimate=pl.CostEstimate(flops=2 * ROWS * D * FF, bytes_accessed=2 * D * FF, transcendentals=0),

time: 108 us -> 106 us (0.981)
  Pallas kernels: 106 us -> 104 us
    pallas_call x1, Pallas kernels: 57.4 us -> 55.7 us  [tail_call(): pl.pallas_call(tail_kernel, out_shape=jax.ShapeDtypeStruct((ROWS, D), BF1...]
where the time goes in v6:
time: 106 us
  Pallas kernels  104 us (98%)
  local copies, waits for them, and re-layouts  1.16 us (1%)
    pallas_call x1, Pallas kernels, tail_call(): pl.pallas_call(tail_kernel, out_shape=jax.ShapeDtypeStruct((ROWS, D), BF1...  55.7 us
    pallas_call x1, Pallas kernels, front_call(): pl.pallas_call(front_kernel, out_shape=(jax.ShapeDtypeStruct((NH + 2, ROW...  24.6 us
    pallas_call x1, Pallas kernels, attn_call(): pl.pallas_call(attn_kernel, out_shape=(jax.ShapeDtypeStruct((NH, ROWS, HD...  23.8 us

profile of v6, /device:TPU:0, one launch (start us, length us, event | category | flops | bytes accessed | tf_op | source)
XLA Modules:
  0.0 106.0 jit_solution(16122242228380293326)
XLA Ops:
  0.6 0.1 maximum_bitcast_fusion.freq
  0.7 0.0 copy-start.1
  0.7 24.6 %front.1 = (f32[50,128,128]{2,1,0:T(8,128)S(1)}, bf16[128,3072]{1,0:T(8,128)(2,1)S(1)}) custom-call(bf16[128,6144]{1,0:T(8,128)(2,1)} %hid.1, f32[1,6144]{1,0:T(1,128)} %bitcast.6, f32[1,6144]{1,0:T(1,128)} %bitcast.7, s32[1,128]{1,0:T(1,128)} %bitcast.5, f32[1,128]{1,0:T(1,128)S(1)} %maximum_bitcast_fusion.freq, bf16[6144,6400]{1,0:T(8,128)(2,1)} %w.1, ...), custom_call_target="tpu_custom_call" | custom-call | flops 6442450944 | bytes 50331648 | tf_op jit(solution)/shard_map/front/pallas_call | solution.py:209
  25.3 0.0 copy-done.1
  25.3 0.0 copy-start
  25.3 23.8 %attn.1 = (f32[48,128,128]{2,1,0:T(8,128)S(1)}, f32[128,128]{1,0:T(8,128)S(1)}, bf16[128,512,128]{2,1,0:T(8,128)(2,1)}, bf16[128,512,128]{2,1,0:T(8,128)(2,1)}) custom-call(s32[128]{0:T(128)S(1)} %copy-done.1, f32[50,128,128]{2,1,0:T(8,128)S(1)} %get-tuple-element.10.qkv, bf16[128,512,128]{2,1,0:T(8,128)(2,1)} %kc.1, bf16[128,512,128]{2,1,0:T(8,128)(2,1)} %vc.1), custom_call_target="tpu_custom_call" | custom-call | flops 1610612736 | bytes 67108864 | tf_op jit(solution)/shard_map/attn/pallas_call | solution.py:318
  49.1 0.0 copy-done
  49.1 55.7 %tail.1 = bf16[128,6144]{1,0:T(8,128)(2,1)S(1)} custom-call(bf16[128,3072]{1,0:T(8,128)(2,1)S(1)} %get-tuple-element.9.act, f32[128,128]{1,0:T(8,128)S(1)} %get-tuple-element.11.ml_in, f32[48,128,128]{2,1,0:T(8,128)S(1)} %get-tuple-element.12.o_in, bf16[128,6144]{1,0:T(8,128)(2,1)S(1)} %copy-done, bf16[3072,6144]{1,0:T(8,128)(2,1)} %w_down.1, ...), custom_call_target="tpu_custom_call" | custom-call | flops 4831838208 | bytes 37748736 | tf_op jit(solution)/shard_map/tail/pallas_call | solution.py:540
  104.8 1.1 %copy.14 = bf16[128,6144]{1,0:T(8,128)(2,1)} copy(bf16[128,6144]{1,0:T(8,128)(2,1)S(1)} %tail.1) | data formatting | bytes 3145728
  (1 shorter events, 0.0 us)
Async XLA Ops:
  0.7 24.6 %copy-start.1 = (s32[128]{0:T(128)S(1)}, s32[128]{0:T(128)}, u32[]{:S(2)}) copy-start(s32[128]{0:T(128)} %pos_ref.1) | copy-start | bytes 1540
  25.3 23.8 %copy-start = (bf16[128,6144]{1,0:T(8,128)(2,1)S(1)}, bf16[128,6144]{1,0:T(8,128)(2,1)}, u32[]{:S(2)}) copy-start(bf16[128,6144]{1,0:T(8,128)(2,1)} %hid.1) | copy-start | bytes 4718596

commit v7 on v6

--- a/solution.py
+++ b/solution.py
@@ -396,6 +396,8 @@
         wts[level, 0] = w1
         wts[level, 1] = w2
         stats[level] = jnp.where(lanes < 64, top, total)
+        if level < 2:
+            m_send(level + 1).start()
 
     def shift(v, by):
         return pltpu.roll(v, lax.rem(HD - by, HD), 1)
@@ -405,8 +407,6 @@
         return here.remote(0, where, where, csend.at[k], crecv.at[k])
 
     def merge_heads(level, k):
-        if k == 0:
-            merge_stats(level)
         o_send(level, k).wait()
         start = own(SIZE[k], level)
         w1 = shift(wts[level, 0], BASE[k] + start)
@@ -416,8 +416,6 @@
             ours = mine[base + h] if level else o_in[BASE[k] + start + h]
             mine[base + h] = ours * w1[:, h:h + 1] + o_to[level][BASE[k] // PART[level] + h] * w2[:, h:h + 1]
         if level < 2:
-            if k == 0:
-                m_send(level + 1).start()
             o_send(level + 1, k).start()
         else:
             l = shift(stats[2], BASE[k] + start)
@@ -497,17 +495,20 @@
     m_send(0).start()
     for k in range(CHUNKS):
         o_send(0, k).start()
+    merge_stats(0)
     for k in range(CHUNKS):
         merge_heads(0, k)
     for s in range(4, W_SLOTS):
         fetch_down(s).start()
     down(0, 1)
+    merge_stats(1)
     merge_heads(1, 0)
     down(1, 3)
     for core in range(2):
         for k in range(CHUNKS):
             wo_copy(core, k).start()
     merge_heads(1, 1)
+    merge_stats(2)
     merge_heads(2, 0)
     down(3, 4)
     merge_heads(1, 2)

time: 106 us -> 106 us (level)
  no operation moved by 1% of the time
where the time goes in v7:
time: 106 us
  Pallas kernels  104 us (98%)
  local copies, waits for them, and re-layouts  1.16 us (1%)
    pallas_call x1, Pallas kernels, tail_call(): pl.pallas_call(tail_kernel, out_shape=jax.ShapeDtypeStruct((ROWS, D), BF1...  55.4 us
    pallas_call x1, Pallas kernels, front_call(): pl.pallas_call(front_kernel, out_shape=(jax.ShapeDtypeStruct((NH + 2, ROW...  24.6 us
    pallas_call x1, Pallas kernels, attn_call(): pl.pallas_call(attn_kernel, out_shape=(jax.ShapeDtypeStruct((NH, ROWS, HD...  23.8 us

profile of v7, /device:TPU:0, one launch (start us, length us, event | category | flops | bytes accessed | tf_op | source)
XLA Modules:
  0.0 105.7 jit_solution(13671045615093463166)
XLA Ops:
  0.6 0.1 maximum_bitcast_fusion.freq
  0.7 0.0 copy-start.1
  0.7 24.6 %front.1 = (f32[50,128,128]{2,1,0:T(8,128)S(1)}, bf16[128,3072]{1,0:T(8,128)(2,1)S(1)}) custom-call(bf16[128,6144]{1,0:T(8,128)(2,1)} %hid.1, f32[1,6144]{1,0:T(1,128)} %bitcast.6, f32[1,6144]{1,0:T(1,128)} %bitcast.7, s32[1,128]{1,0:T(1,128)} %bitcast.5, f32[1,128]{1,0:T(1,128)S(1)} %maximum_bitcast_fusion.freq, bf16[6144,6400]{1,0:T(8,128)(2,1)} %w.1, ...), custom_call_target="tpu_custom_call" | custom-call | flops 6442450944 | bytes 50331648 | tf_op jit(solution)/shard_map/front/pallas_call | solution.py:209
  25.3 0.0 copy-done.1
  25.3 0.0 copy-start
  25.3 23.8 %attn.1 = (f32[48,128,128]{2,1,0:T(8,128)S(1)}, f32[128,128]{1,0:T(8,128)S(1)}, bf16[128,512,128]{2,1,0:T(8,128)(2,1)}, bf16[128,512,128]{2,1,0:T(8,128)(2,1)}) custom-call(s32[128]{0:T(128)S(1)} %copy-done.1, f32[50,128,128]{2,1,0:T(8,128)S(1)} %get-tuple-element.10.qkv, bf16[128,512,128]{2,1,0:T(8,128)(2,1)} %kc.1, bf16[128,512,128]{2,1,0:T(8,128)(2,1)} %vc.1), custom_call_target="tpu_custom_call" | custom-call | flops 1610612736 | bytes 67108864 | tf_op jit(solution)/shard_map/attn/pallas_call | solution.py:318
  49.1 0.0 copy-done
  49.1 55.4 %tail.1 = bf16[128,6144]{1,0:T(8,128)(2,1)S(1)} custom-call(bf16[128,3072]{1,0:T(8,128)(2,1)S(1)} %get-tuple-element.9.act, f32[128,128]{1,0:T(8,128)S(1)} %get-tuple-element.11.ml_in, f32[48,128,128]{2,1,0:T(8,128)S(1)} %get-tuple-element.12.o_in, bf16[128,6144]{1,0:T(8,128)(2,1)S(1)} %copy-done, bf16[3072,6144]{1,0:T(8,128)(2,1)} %w_down.1, ...), custom_call_target="tpu_custom_call" | custom-call | flops 4831838208 | bytes 37748736 | tf_op jit(solution)/shard_map/tail/pallas_call | solution.py:541
  104.6 1.1 %copy.14 = bf16[128,6144]{1,0:T(8,128)(2,1)} copy(bf16[128,6144]{1,0:T(8,128)(2,1)S(1)} %tail.1) | data formatting | bytes 3145728
  (1 shorter events, 0.0 us)
Async XLA Ops:
  0.7 24.6 %copy-start.1 = (s32[128]{0:T(128)S(1)}, s32[128]{0:T(128)}, u32[]{:S(2)}) copy-start(s32[128]{0:T(128)} %pos_ref.1) | copy-start | bytes 1540
  25.3 23.8 %copy-start = (bf16[128,6144]{1,0:T(8,128)(2,1)S(1)}, bf16[128,6144]{1,0:T(8,128)(2,1)}, u32[]{:S(2)}) copy-start(bf16[128,6144]{1,0:T(8,128)(2,1)} %hid.1) | copy-start | bytes 4718596

commit v8 on v7

--- a/solution.py
+++ b/solution.py
@@ -73,6 +73,42 @@
     return pl.ds(BASE[k] // PART[level], SIZE[k] // PART[level])
 
 
+class Spread:
+    COPIES = 6
+
+    def __init__(self, here, ref, base, tiles, send, recv):
+        n = tiles // 8
+        _, a, b = here.sides
+        own, near, far = base + (2 * a + b) * n, base + (2 * a + 1 - b) * n, base + 2 * (1 - a) * n
+        self.spans = ((2, own, n), (1, own, n), (0, own, n), (1, near, n), (0, near, n), (0, far, 2 * n))
+        self.here, self.ref, self.send, self.recv = here, ref, send, recv
+
+    def copy(self, i):
+        level, start, count = self.spans[i]
+        where = self.ref.at[pl.ds(start, count)]
+        return self.here.remote(level, where, where, self.send.at[i], self.recv.at[i])
+
+    def start(self, *which):
+        for i in which:
+            self.copy(i).start()
+
+    def wait(self, *which):
+        for i in which:
+            self.copy(i).wait()
+
+    def step(self, n):
+        if n == 3:
+            self.start(0, 1, 2)
+        elif n == 2:
+            self.wait(0)
+            self.start(3, 4)
+        elif n == 1:
+            self.wait(1, 3)
+            self.start(5)
+        else:
+            self.wait(2, 4, 5)
+
+
 U_SLOTS = 6
 OWN = NH // 8
 UP_STEPS = 12
@@ -131,9 +167,9 @@
     def rotate(v):
         return (v * cos[...] + pltpu.roll(v, HD // 2, 1) * sin[...]).astype(BF16).astype(F32)
 
-    def g_send(level, k):
-        where = qkv.at[pl.ds(BASE[k] + here.own(SIZE[k], level), SIZE[k] // PART[level])]
-        return here.remote(level, where, where, gsend.at[level, k], grecv.at[level, k])
+    def gather(level, k):
+        base = BASE[k] + here.own(SIZE[k], 0)
+        Spread(here, qkv, base, SIZE[k], gsend.at[k], grecv.at[k]).step(level)
 
     def project(weights):
         acc = jnp.dot(normed[...], weights[...], preferred_element_type=F32)
@@ -147,12 +183,7 @@
         for k in chunks:
             for h in range(SIZE[k] // 8):
                 qkv[BASE[k] + here.own(SIZE[k], 2) + h] = rotate(heads[BASE[k] // 8 - first + h])
-            g_send(2, k).start()
-
-    def gather(level, k):
-        g_send(level, k).wait()
-        if level:
-            g_send(level - 1, k).start()
+            gather(3, k)
 
     def up_block(n, carry):
         fetch_up(2 * n).wait()
@@ -222,7 +253,7 @@
             pltpu.VMEM((U_SLOTS, 3072, 512), BF16),
             pltpu.VMEM((ROWS, HD), F32),
             pltpu.VMEM((ROWS, HD), F32),
-            dma((4,)), dma((CHUNKS + 1,)), dma((U_SLOTS,)), dma((LEVELS, CHUNKS)), dma((LEVELS, CHUNKS)),
+            dma((4,)), dma((CHUNKS + 1,)), dma((U_SLOTS,)), dma((CHUNKS, Spread.COPIES)), dma((CHUNKS, Spread.COPIES)),
         ],
         compiler_params=pltpu.CompilerParams(collective_id=0, has_side_effects=True, vmem_limit_bytes=FRONT_LIMIT),
         cost_estimate=pl.CostEstimate(flops=2 * ROWS * D * (FF + 1024), bytes_accessed=2 * D * (FF + 1024), transcendentals=0),
@@ -456,10 +487,6 @@
         src = part.at[pl.ds(here.sides[0] * HALF + 4 * k + other(8, level) - own(8, 0), count)]
         return here.remote(level, src, p_to[level].at[pl.ds(k * count, count)], psend.at[level, k], precv.at[level, k])
 
-    def g_send(level, k):
-        where = gath.at[pl.ds(tile(k, level), 8 // PART[level])]
-        return here.remote(level, where, where, gsend.at[level, k], grecv.at[level, k])
-
     def project(k):
         d_send(k).wait()
         acc = jnp.dot(ctx[...], wobuf[:, k * 512:(k + 1) * 512], preferred_element_type=F32)
@@ -477,13 +504,14 @@
             col = pl.multiple_of(base * HD, HD)
             total = hid[:, pl.ds(col, HD)].astype(F32) + (part[base] + precv2[k])
             gath[base] = total.astype(BF16).astype(F32)
-            g_send(2, k).start()
+            spread(k).step(3)
+
+    def spread(k):
+        return Spread(here, gath, tile(k, 0), 8, gsend.at[k], grecv.at[k])
 
     def gather(level, k):
-        g_send(level, k).wait()
-        if level > 0:
-            g_send(level - 1, k).start()
-        else:
+        spread(k).step(level)
+        if level == 0:
             for t in range(4 * k, 4 * k + 4):
                 for col in (t, HALF + t):
                     out[:, col * HD:(col + 1) * HD] = gath[col].astype(BF16)
@@ -562,7 +590,7 @@
             pltpu.VMEM((ROWS, 2 * OWN * HD), BF16),
             dma((W_SLOTS,)), dma((2, CHUNKS)),
             dma((LEVELS, CHUNKS)), dma((LEVELS, CHUNKS)), dma((LEVELS,)), dma((LEVELS,)), dma((CHUNKS,)), dma((CHUNKS,)),
-            dma((LEVELS, F_CHUNKS)), dma((LEVELS, F_CHUNKS)), dma((LEVELS, F_CHUNKS)), dma((LEVELS, F_CHUNKS)),
+            dma((LEVELS, F_CHUNKS)), dma((LEVELS, F_CHUNKS)), dma((F_CHUNKS, Spread.COPIES)), dma((F_CHUNKS, Spread.COPIES)),
         ],
         compiler_params=pltpu.CompilerParams(collective_id=1, has_side_effects=True, vmem_limit_bytes=TAIL_LIMIT),
         cost_estimate=pl.CostEstimate(flops=2 * ROWS * D * FF, bytes_accessed=2 * D * FF, transcendentals=0),

time: 106 us -> 107 us (level)
    pallas_call x1, Pallas kernels: 24.6 us -> 27.1 us  [front_call(): pl.pallas_call(front_kernel, out_shape=(jax.ShapeDtypeStruct((NH + 2, ROW...]
    pallas_call x1, Pallas kernels: 55.4 us -> 54.3 us  [tail_call(): pl.pallas_call(tail_kernel, out_shape=jax.ShapeDtypeStruct((ROWS, D), BF1...]
where the time goes in v8:
time: 107 us
  Pallas kernels  105 us (98%)
  local copies, waits for them, and re-layouts  1.16 us (1%)
    pallas_call x1, Pallas kernels, tail_call(): pl.pallas_call(tail_kernel, out_shape=jax.ShapeDtypeStruct((ROWS, D), BF1...  54.3 us
    pallas_call x1, Pallas kernels, front_call(): pl.pallas_call(front_kernel, out_shape=(jax.ShapeDtypeStruct((NH + 2, ROW...  27.1 us
    pallas_call x1, Pallas kernels, attn_call(): pl.pallas_call(attn_kernel, out_shape=(jax.ShapeDtypeStruct((NH, ROWS, HD...  23.8 us

profile of v8, /device:TPU:0, one launch (start us, length us, event | category | flops | bytes accessed | tf_op | source)
XLA Modules:
  0.0 107.1 jit_solution(10667160567593244954)
XLA Ops:
  0.6 0.1 maximum_bitcast_fusion.freq
  0.7 0.0 copy-start.1
  0.7 27.1 %front.1 = (f32[50,128,128]{2,1,0:T(8,128)S(1)}, bf16[128,3072]{1,0:T(8,128)(2,1)S(1)}) custom-call(bf16[128,6144]{1,0:T(8,128)(2,1)} %hid.1, f32[1,6144]{1,0:T(1,128)} %bitcast.6, f32[1,6144]{1,0:T(1,128)} %bitcast.7, s32[1,128]{1,0:T(1,128)} %bitcast.5, f32[1,128]{1,0:T(1,128)S(1)} %maximum_bitcast_fusion.freq, bf16[6144,6400]{1,0:T(8,128)(2,1)} %w.1, ...), custom_call_target="tpu_custom_call" | custom-call | flops 6442450944 | bytes 50331648 | tf_op jit(solution)/shard_map/front/pallas_call | solution.py:240
  27.9 0.0 copy-done.1
  27.9 0.0 copy-start
  27.9 23.8 %attn.1 = (f32[48,128,128]{2,1,0:T(8,128)S(1)}, f32[128,128]{1,0:T(8,128)S(1)}, bf16[128,512,128]{2,1,0:T(8,128)(2,1)}, bf16[128,512,128]{2,1,0:T(8,128)(2,1)}) custom-call(s32[128]{0:T(128)S(1)} %copy-done.1, f32[50,128,128]{2,1,0:T(8,128)S(1)} %get-tuple-element.10.qkv, bf16[128,512,128]{2,1,0:T(8,128)(2,1)} %kc.1, bf16[128,512,128]{2,1,0:T(8,128)(2,1)} %vc.1), custom_call_target="tpu_custom_call" | custom-call | flops 1610612736 | bytes 67108864 | tf_op jit(solution)/shard_map/attn/pallas_call | solution.py:349
  51.7 0.0 copy-done
  51.7 54.3 %tail.1 = bf16[128,6144]{1,0:T(8,128)(2,1)S(1)} custom-call(bf16[128,3072]{1,0:T(8,128)(2,1)S(1)} %get-tuple-element.9.act, f32[128,128]{1,0:T(8,128)S(1)} %get-tuple-element.11.ml_in, f32[48,128,128]{2,1,0:T(8,128)S(1)} %get-tuple-element.12.o_in, bf16[128,6144]{1,0:T(8,128)(2,1)S(1)} %copy-done, bf16[3072,6144]{1,0:T(8,128)(2,1)} %w_down.1, ...), custom_call_target="tpu_custom_call" | custom-call | flops 4831838208 | bytes 37748736 | tf_op jit(solution)/shard_map/tail/pallas_call | solution.py:569
  106.0 1.1 %copy.14 = bf16[128,6144]{1,0:T(8,128)(2,1)} copy(bf16[128,6144]{1,0:T(8,128)(2,1)S(1)} %tail.1) | data formatting | bytes 3145728
  (1 shorter events, 0.0 us)
Async XLA Ops:
  0.7 27.2 %copy-start.1 = (s32[128]{0:T(128)S(1)}, s32[128]{0:T(128)}, u32[]{:S(2)}) copy-start(s32[128]{0:T(128)} %pos_ref.1) | copy-start | bytes 1540
  27.9 23.8 %copy-start = (bf16[128,6144]{1,0:T(8,128)(2,1)S(1)}, bf16[128,6144]{1,0:T(8,128)(2,1)}, u32[]{:S(2)}) copy-start(bf16[128,6144]{1,0:T(8,128)(2,1)} %hid.1) | copy-start | bytes 4718596

commit v9 on v7

--- a/solution.py
+++ b/solution.py
@@ -504,13 +504,13 @@
     merge_stats(1)
     merge_heads(1, 0)
     down(1, 3)
-    for core in range(2):
-        for k in range(CHUNKS):
-            wo_copy(core, k).start()
     merge_heads(1, 1)
     merge_stats(2)
     merge_heads(2, 0)
     down(3, 4)
+    for core in range(2):
+        for k in range(CHUNKS):
+            wo_copy(core, k).start()
     merge_heads(1, 2)
     down(4, 5)
     merge_heads(1, 3)

time: 106 us -> 106 us (level)
  no operation moved by 1% of the time
where the time goes in v9:
time: 106 us
  Pallas kernels  104 us (98%)
  local copies, waits for them, and re-layouts  1.16 us (1%)
    pallas_call x1, Pallas kernels, tail_call(): pl.pallas_call(tail_kernel, out_shape=jax.ShapeDtypeStruct((ROWS, D), BF1...  55.4 us
    pallas_call x1, Pallas kernels, front_call(): pl.pallas_call(front_kernel, out_shape=(jax.ShapeDtypeStruct((NH + 2, ROW...  24.6 us
    pallas_call x1, Pallas kernels, attn_call(): pl.pallas_call(attn_kernel, out_shape=(jax.ShapeDtypeStruct((NH, ROWS, HD...  23.8 us

profile of v9, /device:TPU:0, one launch (start us, length us, event | category | flops | bytes accessed | tf_op | source)
XLA Modules:
  0.0 105.7 jit_solution(15426757008983273112)
XLA Ops:
  0.6 0.1 maximum_bitcast_fusion.freq
  0.7 0.0 copy-start.1
  0.7 24.6 %front.1 = (f32[50,128,128]{2,1,0:T(8,128)S(1)}, bf16[128,3072]{1,0:T(8,128)(2,1)S(1)}) custom-call(bf16[128,6144]{1,0:T(8,128)(2,1)} %hid.1, f32[1,6144]{1,0:T(1,128)} %bitcast.6, f32[1,6144]{1,0:T(1,128)} %bitcast.7, s32[1,128]{1,0:T(1,128)} %bitcast.5, f32[1,128]{1,0:T(1,128)S(1)} %maximum_bitcast_fusion.freq, bf16[6144,6400]{1,0:T(8,128)(2,1)} %w.1, ...), custom_call_target="tpu_custom_call" | custom-call | flops 6442450944 | bytes 50331648 | tf_op jit(solution)/shard_map/front/pallas_call | solution.py:209
  25.3 0.0 copy-done.1
  25.3 0.0 copy-start
  25.3 23.8 %attn.1 = (f32[48,128,128]{2,1,0:T(8,128)S(1)}, f32[128,128]{1,0:T(8,128)S(1)}, bf16[128,512,128]{2,1,0:T(8,128)(2,1)}, bf16[128,512,128]{2,1,0:T(8,128)(2,1)}) custom-call(s32[128]{0:T(128)S(1)} %copy-done.1, f32[50,128,128]{2,1,0:T(8,128)S(1)} %get-tuple-element.10.qkv, bf16[128,512,128]{2,1,0:T(8,128)(2,1)} %kc.1, bf16[128,512,128]{2,1,0:T(8,128)(2,1)} %vc.1), custom_call_target="tpu_custom_call" | custom-call | flops 1610612736 | bytes 67108864 | tf_op jit(solution)/shard_map/attn/pallas_call | solution.py:318
  49.1 0.0 copy-done
  49.1 55.4 %tail.1 = bf16[128,6144]{1,0:T(8,128)(2,1)S(1)} custom-call(bf16[128,3072]{1,0:T(8,128)(2,1)S(1)} %get-tuple-element.9.act, f32[128,128]{1,0:T(8,128)S(1)} %get-tuple-element.11.ml_in, f32[48,128,128]{2,1,0:T(8,128)S(1)} %get-tuple-element.12.o_in, bf16[128,6144]{1,0:T(8,128)(2,1)S(1)} %copy-done, bf16[3072,6144]{1,0:T(8,128)(2,1)} %w_down.1, ...), custom_call_target="tpu_custom_call" | custom-call | flops 4831838208 | bytes 37748736 | tf_op jit(solution)/shard_map/tail/pallas_call | solution.py:541
  104.6 1.1 %copy.14 = bf16[128,6144]{1,0:T(8,128)(2,1)} copy(bf16[128,6144]{1,0:T(8,128)(2,1)S(1)} %tail.1) | data formatting | bytes 3145728
  (1 shorter events, 0.0 us)
Async XLA Ops:
  0.7 24.6 %copy-start.1 = (s32[128]{0:T(128)S(1)}, s32[128]{0:T(128)}, u32[]{:S(2)}) copy-start(s32[128]{0:T(128)} %pos_ref.1) | copy-start | bytes 1540
  25.3 23.8 %copy-start = (bf16[128,6144]{1,0:T(8,128)(2,1)S(1)}, bf16[128,6144]{1,0:T(8,128)(2,1)}, u32[]{:S(2)}) copy-start(bf16[128,6144]{1,0:T(8,128)(2,1)} %hid.1) | copy-start | bytes 4718596
